TPU v7x, 256 devices: a whole 4x4x8 slice. The times are simulated.
256 devices in a mesh: cfg: 64 (over z, x_lo, y), lat: 4 (over x_hi, core).
Axes of the slice: x: 4 (x_hi: 2, x_lo: 2; x = x_hi * 2 + x_lo), y: 4, z: 8, core: 2. Of those that a mesh axis runs over, the one named last changes fastest.
Arguments:
- latent_mode: float32 [128, 1048576], P('cfg', 'lat'), may hold values from -6 to 6
- latent_var: float32 [128, 1048576], P('cfg', 'lat'), may hold values from 0.05 to 2
- config_weight: float32 [128], P('cfg'), may hold values from 0.05 to 20
- grid_offset: float32 [64], replicated, may hold values from -3 to 3
Outputs:
- marginal_density: float32 [64, 1048576], P(None, ('cfg', 'lat'))
- marginal_moments: float32 [2, 1048576], P(None, ('cfg', 'lat'))
All inputs are finite; a program needn't handle non-finite values.
Results may differ from a plain program's by a relative error of at most 0.00002.
Values sent between devices are 32-bit elements; how exact they have to be, the bound alone decides.
A program may use at most 64 MiB of HBM per device.

v0:
```python
import jax
import jax.numpy as jnp
from jax import lax
from jax.sharding import PartitionSpec as P


def sent_to_all(shard, axis):
    copies = jnp.broadcast_to(shard, (lax.axis_size(axis), *shard.shape))
    return lax.all_to_all(copies, axis, split_axis=0, concat_axis=0, tiled=True)


def in_order(blocks, dim):
    blocks = jnp.moveaxis(blocks, 0, dim)
    lengths = blocks.shape
    return blocks.reshape(*lengths[:dim], lengths[dim] * lengths[dim + 1], *lengths[dim + 2 :])


def gathered_copies(shard, axis, dim):
    blocks = sent_to_all(shard, axis)
    return in_order(blocks, dim)


def grouped_exchange(shard, axis, split_dim, concat_dim, work, item_dim, out_dim):

    def moved(group):
        return lax.all_to_all(group, axis, split_axis=split_dim, concat_axis=concat_dim, tiled=True)

    items = jax.tree.leaves(shard)[0].shape[item_dim]
    ends = [items * k // 2 for k in range(2 + 1)] if items % 2 == 0 else [0, items]
    groups = [
        jax.tree.map(lambda a: lax.slice_in_dim(a, low, high, axis=item_dim), shard)
        for low, high in zip(ends, ends[1:])
    ]
    arrived = [moved(group) for group in groups]
    made = [work(group) for group in arrived]
    return jax.tree.map(lambda *parts: jnp.concatenate(parts, axis=out_dim), *made)


def mixture(mode_block, var_block, norm_weight, grid_offset):
    centre = jnp.sum(norm_weight[:, None] * mode_block, axis=0)
    deviation = mode_block - centre[None, :]
    spread = jnp.sqrt(jnp.sum(norm_weight[:, None] * (var_block + deviation * deviation), axis=0))
    points = centre[None, :] + grid_offset[:, None] * spread[None, :]
    coefficient = norm_weight[:, None] / jnp.sqrt(6.283185307179586 * var_block)
    precision = 1.0 / var_block
    gap = points[None, :, :] - mode_block[:, None, :]
    terms = coefficient[:, None, :] * jnp.exp(-0.5 * gap * gap * precision[:, None, :])
    density = spread[None, :] * jnp.sum(terms, axis=0)
    return (density, jnp.stack([centre, spread], axis=0))


def evaluate(packed, norm_weight, grid_offset):
    blocks_first = jnp.moveaxis(packed, 2, 0)

    def one_block(block_data):
        return mixture(block_data[0], block_data[1], norm_weight, grid_offset)

    density, moments = lax.map(one_block, blocks_first)
    return (jnp.moveaxis(density, 0, 1), jnp.moveaxis(moments, 0, 1))


def per_device(latent_mode, latent_var, config_weight, grid_offset):
    all_weights = gathered_copies(config_weight, "cfg", 0)
    norm_weight = all_weights / jnp.sum(all_weights)
    n_cfg = lax.axis_size("cfg")
    n_lat = lax.axis_size("lat")
    groups = n_cfg // n_lat
    own_cfg = latent_mode.shape[0]
    lat_dev = latent_mode.shape[1] // n_cfg
    width = min(lat_dev, 512)
    count = lat_dev // width
    packed = jnp.stack([latent_mode, latent_var], axis=0)
    packed = packed.reshape(2, own_cfg, groups, n_lat, lat_dev)
    first = lax.all_to_all(packed, "lat", split_axis=3, concat_axis=2, tiled=True)
    first = first.reshape(2, own_cfg, n_cfg, count, width)

    def arrived(pieces):
        total_cfg = pieces.shape[1] * pieces.shape[2]
        items = pieces.shape[3]
        return evaluate(pieces.reshape(2, total_cfg, items, width), norm_weight, grid_offset)

    density, moments = grouped_exchange(first, "cfg", 2, 1, arrived, 3, 1)
    density = density.reshape(density.shape[0], lat_dev)
    moments = moments.reshape(2, lat_dev)
    return (density, moments)


def solution(mesh):
    return jax.shard_map(
        per_device,
        mesh=mesh,
        in_specs=(P("cfg", "lat"), P("cfg", "lat"), P("cfg"), P()),
        out_specs=(P(None, ("cfg", "lat")), P(None, ("cfg", "lat"))),
        check_vma=False,
    )
```

profile of v0, /device:TPU:1, one launch (start us, length us, event | category | flops | bytes accessed | tf_op | source)
XLA Modules:
  0.0 231.5 jit_solution(10533520981784114635)
XLA Ops:
  0.6 3.7 %stack.19 = f32[1,2,16,4,4096]{4,3,2,1,0:T(4,128)S(1)} reshape(f32[2,262144]{1,0:T(2,128)} %param.8) | data formatting | bytes 4194304 | tf_op jit(solution)/shard_map/stack | solution.py:72
  4.4 5.1 %stack.20 = f32[1,2,16,4,4096]{4,3,2,1,0:T(4,128)} reshape(f32[2,262144]{1,0:T(2,128)} %param.9) | data formatting | bytes 4194304 | tf_op jit(solution)/shard_map/stack | solution.py:72
  9.5 2.7 %pad_maximum_fusion = f32[2,2,16,4,4096]{4,3,2,1,0:T(4,128)S(1)} fusion(f32[1,2,16,4,4096]{4,3,2,1,0:T(4,128)} %stack.20, f32[1,2,16,4,4096]{4,3,2,1,0:T(4,128)S(1)} %stack.19), kind=kLoop, calls=%fused_computation.36 | loop fusion | flops 1048576 | bytes 8388608 | tf_op jit(solution)/shard_map/stack | solution.py:72
  12.2 2.4 %copy.39 = f32[2,2,16,4,4096]{4,2,1,0,3:T(8,128)S(1)} copy(f32[2,2,16,4,4096]{4,3,2,1,0:T(4,128)S(1)} %pad_maximum_fusion) | data formatting | bytes 8388608 | tf_op jit(solution)/shard_map/stack | solution.py:72
  14.6 55.2 %all_to_all.51 = f32[2,2,16,4,4096]{4,2,1,0,3:T(8,128)} all-to-all(f32[2,2,16,4,4096]{4,2,1,0,3:T(8,128)S(1)} %copy.39), channel_id=1, replica_groups=mesh['cfg'=64,'lat'=4] {'lat'}, dimensions={3} | all-to-all | bytes 8388608 | tf_op jit(solution)/shard_map/all_to_all | solution.py:74
  70.5 11.2 %all-to-all-start = ((f32[64,1,2]{2,1,0:T(1,128)}), f32[64,1,2]{2,1,0:T(1,128)S(1)}, u32[]{:S(2)}, u32[]{:S(2)}) async-start(f32[64,1,2]{2,1,0:T(1,128)} %broadcast_in_dim.27), calls=%async_computation | async-start | bytes 65536 | tf_op jit(solution)/shard_map/all_to_all | solution.py:9
  81.7 2.5 %copy.40 = f32[2,2,4,16,1,4096]{5,3,2,1,0,4:T(8,128)S(1)} copy(f32[2,2,4,16,1,4096]{5,3,1,0,2,4:T(8,128)} %bitcast.107) | data formatting | bytes 8388608 | tf_op jit(solution)/shard_map/all_to_all | solution.py:74
  84.2 3.8 %copy.56 = f32[32,8,8,512]{3,2,1,0:T(8,128)S(1)} copy(f32[32,8,8,512]{3,1,2,0:T(8,128)S(1)} %bitcast.109) | data formatting | bytes 8388608
  92.0 10.5 %all-to-all-start.2 = ((f32[2,2,64,4,512]{4,3,1,0,2:T(4,128)}), f32[2,2,64,4,512]{4,3,1,0,2:T(4,128)S(1)}, u32[]{:S(2)}, u32[]{:S(2)}) async-start(f32[2,2,64,4,512]{4,3,1,0,2:T(4,128)} %copy.41), calls=%async_computation.2 | async-start | bytes 4194304 | tf_op jit(solution)/shard_map/all_to_all | solution.py:26
  104.2 3.6 %copy.44 = f32[2,2,64,4,512]{4,3,1,0,2:T(4,128)} copy(f32[2,2,64,4,512]{4,3,2,1,0:T(4,128)} %get-tuple-element.155) | data formatting | bytes 4194304 | tf_op jit(solution)/shard_map/slice | solution.py:31
  107.8 42.2 %all-to-all-done.2 = f32[2,2,64,4,512]{4,3,1,0,2:T(4,128)S(1)} async-done(((f32[2,2,64,4,512]{4,3,1,0,2:T(4,128)}), f32[2,2,64,4,512]{4,3,1,0,2:T(4,128)S(1)}, u32[]{:S(2)}, u32[]{:S(2)}) %all-to-all-start.2) | async-done | bytes 2097184 | tf_op jit(solution)/shard_map/all_to_all | solution.py:26
  150.0 9.2 %all-to-all-start.3 = ((f32[2,2,64,4,512]{4,3,1,0,2:T(4,128)}), f32[2,2,64,4,512]{4,3,1,0,2:T(4,128)}, u32[]{:S(2)}, u32[]{:S(2)}) async-start(f32[2,2,64,4,512]{4,3,1,0,2:T(4,128)} %copy.44), calls=%async_computation.3 | async-start | bytes 4194304 | tf_op jit(solution)/shard_map/all_to_all | solution.py:26
  159.1 2.1 copy.42
  161.3 21.1 %while.24 = (s32[]{:T(128)}, f32[4,64,512]{2,1,0:T(8,128)S(1)}, f32[4,2,512]{2,1,0:T(2,128)S(1)}, f32[128]{0:T(128)S(1)}, f32[4,2,128,512]{3,0,2,1:T(4,128)S(1)}...) while((s32[]{:T(128)}, f32[4,64,512]{2,1,0:T(8,128)S(1)}, f32[4,2,512]{2,1,0:T(2,128)S(1)}, ...), condition=%wide.region_5.6_spmd, body=%wide.region_1.5_spmd.sunk | while | flops 25886724 | bytes 4351353 | solution.py:58
  162.2 4.4 %fusion.21 = f32[64,512]{1,0:T(8,128)S(1)} fusion(f32[128,512]{1,0:T(8,128)S(1)} %get-tuple-element.236, f32[128,512]{1,0:T(8,128)S(1)} %bitcast.113, f32[64,512]{1,0:T(8,128)S(1)} %multiply_add_fusion.4, f32[128,512]{1,0:T(8,128)S(1)} %get-tuple-element.238), kind=kLoop, calls=%fused_computation.4.clone.1 | loop fusion | flops 25133056 | bytes 1048576 | tf_op jit(solution)/shard_map/while/body/eval_jaxpr/reduce_sum | solution.py:48
  167.4 4.4 %fusion.21 = f32[64,512]{1,0:T(8,128)S(1)} fusion(f32[128,512]{1,0:T(8,128)S(1)} %get-tuple-element.236, f32[128,512]{1,0:T(8,128)S(1)} %bitcast.113, f32[64,512]{1,0:T(8,128)S(1)} %multiply_add_fusion.4, f32[128,512]{1,0:T(8,128)S(1)} %get-tuple-element.238), kind=kLoop, calls=%fused_computation.4.clone.1 | loop fusion | flops 25133056 | bytes 1048576 | tf_op jit(solution)/shard_map/while/body/eval_jaxpr/reduce_sum | solution.py:48
  172.7 4.4 %fusion.21 = f32[64,512]{1,0:T(8,128)S(1)} fusion(f32[128,512]{1,0:T(8,128)S(1)} %get-tuple-element.236, f32[128,512]{1,0:T(8,128)S(1)} %bitcast.113, f32[64,512]{1,0:T(8,128)S(1)} %multiply_add_fusion.4, f32[128,512]{1,0:T(8,128)S(1)} %get-tuple-element.238), kind=kLoop, calls=%fused_computation.4.clone.1 | loop fusion | flops 25133056 | bytes 1048576 | tf_op jit(solution)/shard_map/while/body/eval_jaxpr/reduce_sum | solution.py:48
  178.0 4.4 %fusion.21 = f32[64,512]{1,0:T(8,128)S(1)} fusion(f32[128,512]{1,0:T(8,128)S(1)} %get-tuple-element.236, f32[128,512]{1,0:T(8,128)S(1)} %bitcast.113, f32[64,512]{1,0:T(8,128)S(1)} %multiply_add_fusion.4, f32[128,512]{1,0:T(8,128)S(1)} %get-tuple-element.238), kind=kLoop, calls=%fused_computation.4.clone.1 | loop fusion | flops 25133056 | bytes 1048576 | tf_op jit(solution)/shard_map/while/body/eval_jaxpr/reduce_sum | solution.py:48
  182.5 24.0 %all-to-all-done.3 = f32[2,2,64,4,512]{4,3,1,0,2:T(4,128)} async-done(((f32[2,2,64,4,512]{4,3,1,0,2:T(4,128)}), f32[2,2,64,4,512]{4,3,1,0,2:T(4,128)}, u32[]{:S(2)}, u32[]{:S(2)}) %all-to-all-start.3) | async-done | bytes 2097184 | tf_op jit(solution)/shard_map/all_to_all | solution.py:26
  208.6 21.1 %while.25 = (s32[]{:T(128)}, f32[4,64,512]{2,1,0:T(8,128)S(1)}, f32[4,2,512]{2,1,0:T(2,128)S(1)}, f32[128]{0:T(128)S(1)}, f32[4,2,128,512]{3,0,2,1:T(4,128)S(1)}...) while((s32[]{:T(128)}, f32[4,64,512]{2,1,0:T(8,128)S(1)}, f32[4,2,512]{2,1,0:T(2,128)S(1)}, ...), condition=%wide.region_10.11_spmd, body=%wide.region_6.10_spmd.sunk | while | flops 25886724 | bytes 4351353 | solution.py:58
  209.4 4.4 %fusion.24 = f32[64,512]{1,0:T(8,128)S(1)} fusion(f32[128,512]{1,0:T(8,128)S(1)} %get-tuple-element.247, f32[128,512]{1,0:T(8,128)S(1)} %bitcast.114, f32[64,512]{1,0:T(8,128)S(1)} %multiply_add_fusion.5, f32[128,512]{1,0:T(8,128)S(1)} %get-tuple-element.249), kind=kLoop, calls=%fused_computation.22.clone.1 | loop fusion | flops 25133056 | bytes 1048576 | tf_op jit(solution)/shard_map/while/body/eval_jaxpr/reduce_sum | solution.py:48
  214.7 4.4 %fusion.24 = f32[64,512]{1,0:T(8,128)S(1)} fusion(f32[128,512]{1,0:T(8,128)S(1)} %get-tuple-element.247, f32[128,512]{1,0:T(8,128)S(1)} %bitcast.114, f32[64,512]{1,0:T(8,128)S(1)} %multiply_add_fusion.5, f32[128,512]{1,0:T(8,128)S(1)} %get-tuple-element.249), kind=kLoop, calls=%fused_computation.22.clone.1 | loop fusion | flops 25133056 | bytes 1048576 | tf_op jit(solution)/shard_map/while/body/eval_jaxpr/reduce_sum | solution.py:48
  220.0 4.4 %fusion.24 = f32[64,512]{1,0:T(8,128)S(1)} fusion(f32[128,512]{1,0:T(8,128)S(1)} %get-tuple-element.247, f32[128,512]{1,0:T(8,128)S(1)} %bitcast.114, f32[64,512]{1,0:T(8,128)S(1)} %multiply_add_fusion.5, f32[128,512]{1,0:T(8,128)S(1)} %get-tuple-element.249), kind=kLoop, calls=%fused_computation.22.clone.1 | loop fusion | flops 25133056 | bytes 1048576 | tf_op jit(solution)/shard_map/while/body/eval_jaxpr/reduce_sum | solution.py:48
  225.3 4.4 %fusion.24 = f32[64,512]{1,0:T(8,128)S(1)} fusion(f32[128,512]{1,0:T(8,128)S(1)} %get-tuple-element.247, f32[128,512]{1,0:T(8,128)S(1)} %bitcast.114, f32[64,512]{1,0:T(8,128)S(1)} %multiply_add_fusion.5, f32[128,512]{1,0:T(8,128)S(1)} %get-tuple-element.249), kind=kLoop, calls=%fused_computation.22.clone.1 | loop fusion | flops 25133056 | bytes 1048576 | tf_op jit(solution)/shard_map/while/body/eval_jaxpr/reduce_sum | solution.py:48
  (85 shorter events, 16.8 us)
Async XLA Ops:
  14.6 55.2 %copy-start.2 = (f32[2]{0:T(128)S(1)}, f32[2]{0:T(128)}, u32[]{:S(2)}) copy-start(f32[2]{0:T(128)} %param.10) | copy-start | bytes 28
  70.5 21.5 %all-to-all-start = ((f32[64,1,2]{2,1,0:T(1,128)}), f32[64,1,2]{2,1,0:T(1,128)S(1)}, u32[]{:S(2)}, u32[]{:S(2)}) async-start(f32[64,1,2]{2,1,0:T(1,128)} %broadcast_in_dim.27), calls=%async_computation | async-start | bytes 65536 | tf_op jit(solution)/shard_map/all_to_all | solution.py:9
  92.0 58.0 %all-to-all-start.2 = ((f32[2,2,64,4,512]{4,3,1,0,2:T(4,128)}), f32[2,2,64,4,512]{4,3,1,0,2:T(4,128)S(1)}, u32[]{:S(2)}, u32[]{:S(2)}) async-start(f32[2,2,64,4,512]{4,3,1,0,2:T(4,128)} %copy.41), calls=%async_computation.2 | async-start | bytes 4194304 | tf_op jit(solution)/shard_map/all_to_all | solution.py:26
  107.8 53.6 %copy-start.1 = (f32[64]{0:T(128)S(1)}, f32[64]{0:T(128)}, u32[]{:S(2)}) copy-start(f32[64]{0:T(128)} %param.11) | copy-start | bytes 772
  150.0 9.2 %copy-start = (f32[2,2,64,4,512]{4,3,1,0,2:T(4,128)}, f32[2,2,64,4,512]{4,3,1,0,2:T(4,128)S(1)}, u32[]{:S(2)}) copy-start(f32[2,2,64,4,512]{4,3,1,0,2:T(4,128)S(1)} %all-to-all-done.2) | copy-start | bytes 6291460
  150.0 56.5 %all-to-all-start.3 = ((f32[2,2,64,4,512]{4,3,1,0,2:T(4,128)}), f32[2,2,64,4,512]{4,3,1,0,2:T(4,128)}, u32[]{:S(2)}, u32[]{:S(2)}) async-start(f32[2,2,64,4,512]{4,3,1,0,2:T(4,128)} %copy.44), calls=%async_computation.3 | async-start | bytes 4194304 | tf_op jit(solution)/shard_map/all_to_all | solution.py:26
where the time goes:
time: 234 us; the launch traced here: 231 us
  waiting for transfers between devices  66.1 us (28%)
  blocking collectives  55.2 us (24%)
  other arithmetic  42.8 us (18%)
  local copies, waits for them, and re-layouts  35.1 us (15%)
  starting transfers between devices  30.9 us (13%)
    all_to_all x2, waiting for transfers between devices, moved(): lax.all_to_all(group, axis, split_axis=split_dim, concat_axis=concat_dim,...  66.1 us
    all_to_all x1, blocking collectives, per_device(): lax.all_to_all(packed, 'lat', split_axis=3, concat_axis=2, tiled=True)  55.2 us
    reduce_sum x8, other arithmetic, mixture(): density = spread[None, :] * jnp.sum(terms, axis=0)  35.2 us
    all_to_all x2, starting transfers between devices, moved(): lax.all_to_all(group, axis, split_axis=split_dim, concat_axis=concat_dim,...  19.6 us
    another operation x3, local copies, waits for them, and re-layouts, per_device(): packed = jnp.stack([latent_mode, latent_var], axis=0)  11.3 us
    all_to_all x1, starting transfers between devices, sent_to_all(): return lax.all_to_all(copies, axis, split_axis=0, concat_axis=0, tiled=True)  11.2 us
    slice x3, local copies, waits for them, and re-layouts, grouped_exchange(): lax.slice_in_dim(a, low, high, axis=item_dim)  7.62 us
  transfers between devices with their start and end apart: 3, of which 2 were waited for; matrix products, arithmetic and copies ran while one was open for 17% of the time, Pallas kernels for 0%

commit v1 on v0

v1 whole, which is shorter than its diff:
```python
import functools
import math

import jax
import jax.numpy as jnp
from jax import lax
from jax.experimental import pallas as pl
from jax.experimental.pallas import tpu as pltpu
from jax.sharding import PartitionSpec as P

MESH = pl.DeviceIdType.MESH
LANES = 128
CHUNKS = 4
AHEAD = 2
GROUP = 16
LOG2E = 1.4426950408889634


def pair_sum(x, even):
    return x + jnp.where(even, pltpu.roll(x, 7, 0), pltpu.roll(x, 1, 0))


def kernel(n_cfg, n_lat, mode, var, weight, offset, dens, mom, buf, wbuf, wnorm, coef, send_sem, recv_sem, wsend_sem, wrecv_sem):
    c = lax.axis_index("cfg")
    l = lax.axis_index("lat")
    dests = n_cfg
    rows = mode.shape[0] // dests
    size = rows // CHUNKS
    near = n_cfg // n_lat
    first = l * near
    turn = lax.rem(c * 4 + l, dests)

    def target(i):
        d = lax.rem(i + turn, dests)
        return d, first + d // n_lat, lax.rem(d, n_lat)

    def each(i, do_local, do_remote):
        d, tc, tl = target(i)
        own = jnp.logical_and(tc == c, tl == l)

        @pl.when(own)
        def _():
            do_local(d)

        @pl.when(jnp.logical_not(own))
        def _():
            do_remote(d, tc, tl)

    def send_weights(i, carry):
        def local(d):
            pltpu.make_async_copy(weight, wbuf.at[c], wrecv_sem).start()

        def remote(d, tc, tl):
            pltpu.make_async_remote_copy(
                src_ref=weight, dst_ref=wbuf.at[c], send_sem=wsend_sem, recv_sem=wrecv_sem,
                device_id=(tc, tl), device_id_type=MESH,
            ).start()

        each(i, local, remote)
        return carry

    def send_chunk(j):
        def body(i, carry):
            def src(ref, d):
                return ref.at[pl.ds(pl.multiple_of(d * rows + j * size, 8), size)]

            def local(d):
                for a, ref in enumerate((mode, var)):
                    pltpu.make_async_copy(src(ref, d), buf.at[j, a, c], recv_sem.at[j]).start()

            def remote(d, tc, tl):
                for a, ref in enumerate((mode, var)):
                    pltpu.make_async_remote_copy(
                        src_ref=src(ref, d), dst_ref=buf.at[j, a, c], send_sem=send_sem.at[j], recv_sem=recv_sem.at[j],
                        device_id=(tc, tl), device_id_type=MESH,
                    ).start()

            each(i, local, remote)
            return carry

        lax.fori_loop(0, dests, body, 0)

    lax.fori_loop(0, dests, send_weights, 0)
    for j in range(min(AHEAD, CHUNKS)):
        send_chunk(j)

    parity = lax.broadcasted_iota(jnp.int32, (8, LANES), 0)
    even = lax.rem(parity, 2) == 0

    pltpu.make_async_copy(wbuf, wbuf, wrecv_sem).wait()

    def spread_weight(s, total):
        w = jnp.where(even, jnp.broadcast_to(wbuf[s, 0:1, :], (8, LANES)), jnp.broadcast_to(wbuf[s, 1:2, :], (8, LANES)))
        wnorm[s] = w
        return total + w

    total = lax.fori_loop(0, n_cfg, spread_weight, jnp.zeros((8, LANES), jnp.float32), unroll=8)
    total = pair_sum(total, even)

    def divide_weight(s, carry):
        wnorm[s] = wnorm[s] / total
        return carry

    lax.fori_loop(0, n_cfg, divide_weight, 0, unroll=8)

    zero = jnp.zeros((8, LANES), jnp.float32)
    for j in range(CHUNKS):
        pltpu.make_async_copy(buf.at[j], buf.at[j], recv_sem.at[j]).wait()

        def tile(q, carry):
            at = pl.ds(pl.multiple_of(q * 8, 8), 8)

            def first_moment(s, acc):
                return acc + wnorm[s] * buf[j, 0, s, at, :]

            centre = pair_sum(lax.fori_loop(0, n_cfg, first_moment, zero, unroll=8), even)

            def second_moment(s, acc):
                dev = buf[j, 0, s, at, :] - centre
                return acc + wnorm[s] * (buf[j, 1, s, at, :] + dev * dev)

            spread = jnp.sqrt(pair_sum(lax.fori_loop(0, n_cfg, second_moment, zero, unroll=8), even))

            def prepare(s, carry):
                root = lax.rsqrt(buf[j, 1, s, at, :])
                scale = root * math.sqrt(0.5 * LOG2E)
                coef[0, s] = scale * (centre - buf[j, 0, s, at, :])
                coef[1, s] = scale * spread
                coef[2, s] = wnorm[s] * root * (1.0 / math.sqrt(2.0 * math.pi))
                return carry

            lax.fori_loop(0, n_cfg, prepare, 0, unroll=8)

            column = (j * size + q * 8) * (LANES // 2)
            for t in range(4):
                lanes = pl.ds(pl.multiple_of(column + t * LANES, LANES), LANES)
                mom[0:1, lanes] = centre[2 * t : 2 * t + 1, :]
                mom[1:2, lanes] = spread[2 * t : 2 * t + 1, :]

            for base in range(0, dens.shape[0], GROUP):
                grid = [jnp.full((8, LANES), offset[base + g], jnp.float32) for g in range(GROUP)]

                def add_source(s, accs):
                    a, b, k = coef[0, s], coef[1, s], coef[2, s]
                    out = []
                    for g in range(GROUP):
                        x = a + grid[g] * b
                        out.append(accs[g] + k * jnp.exp2(-(x * x)))
                    return tuple(out)

                accs = lax.fori_loop(0, n_cfg, add_source, (zero,) * GROUP, unroll=2)
                for g in range(GROUP):
                    value = spread * pair_sum(accs[g], even)
                    for t in range(4):
                        lanes = pl.ds(pl.multiple_of(column + t * LANES, LANES), LANES)
                        dens[base + g : base + g + 1, lanes] = value[2 * t : 2 * t + 1, :]
            return carry

        if j + AHEAD < CHUNKS:
            send_chunk(j + AHEAD)
        lax.fori_loop(0, size // 8, tile, 0)

    def finish(i, carry):
        _, tc, tl = target(i)
        own = jnp.logical_and(tc == c, tl == l)

        @pl.when(jnp.logical_not(own))
        def _():
            pltpu.make_async_copy(weight, wbuf.at[0], wsend_sem).wait()
            for j in range(CHUNKS):
                pltpu.make_async_copy(buf.at[j, :, 0], buf.at[j, :, 0], send_sem.at[j]).wait()

        return carry

    lax.fori_loop(0, dests, finish, 0)


def per_device(latent_mode, latent_var, config_weight, grid_offset):
    n_cfg = lax.axis_size("cfg")
    n_lat = lax.axis_size("lat")
    own, width = latent_mode.shape
    grid = grid_offset.shape[0]
    lat_dev = width // n_cfg

    def rows(a):
        return a.reshape(own, width // LANES, LANES).transpose(1, 0, 2).reshape(own * width // LANES, LANES)

    weight = jnp.broadcast_to(config_weight[:, None], (own, LANES))
    block = own * lat_dev // LANES
    vmem = pl.BlockSpec(memory_space=pltpu.VMEM)
    hbm = pl.BlockSpec(memory_space=pl.ANY)
    return pl.pallas_call(
        functools.partial(kernel, n_cfg, n_lat),
        out_shape=(
            jax.ShapeDtypeStruct((grid, lat_dev), jnp.float32),
            jax.ShapeDtypeStruct((2, lat_dev), jnp.float32),
        ),
        in_specs=[hbm, hbm, vmem, pl.BlockSpec(memory_space=pltpu.SMEM)],
        out_specs=(vmem, vmem),
        scratch_shapes=[
            pltpu.VMEM((CHUNKS, 2, n_cfg, block // CHUNKS, LANES), jnp.float32),
            pltpu.VMEM((n_cfg, own, LANES), jnp.float32),
            pltpu.VMEM((n_cfg, 8, LANES), jnp.float32),
            pltpu.VMEM((3, n_cfg, 8, LANES), jnp.float32),
            pltpu.SemaphoreType.DMA((CHUNKS,)),
            pltpu.SemaphoreType.DMA((CHUNKS,)),
            pltpu.SemaphoreType.DMA,
            pltpu.SemaphoreType.DMA,
        ],
        compiler_params=pltpu.CompilerParams(has_side_effects=True, vmem_limit_bytes=40 * 1024 * 1024),
        name="mixture",
    )(rows(latent_mode), rows(latent_var), weight, grid_offset)


def solution(mesh):
    return jax.shard_map(
        per_device,
        mesh=mesh,
        in_specs=(P("cfg", "lat"), P("cfg", "lat"), P("cfg"), P()),
        out_specs=(P(None, ("cfg", "lat")), P(None, ("cfg", "lat"))),
        check_vma=False,
    )
```

time: 234 us -> 240 us (1.026)
  the two profiles are of different devices: /device:TPU:1 before, /device:TPU:195 now
where the time goes in v1:
time: 240 us
  Pallas kernels  233 us (97%)
  local copies, waits for them, and re-layouts  6.15 us (3%)
    pallas_call x1, Pallas kernels, per_device(): pl.pallas_call(functools.partial(kernel, n_cfg, n_lat), out_shape=(jax.Sh...  233 us
    unnamed x8, local copies, waits for them, and re-layouts  5.42 us

profile of v1, /device:TPU:195, one launch (start us, length us, event | category | flops | bytes accessed | tf_op | source)
XLA Modules:
  0.0 240.1 jit_solution(14665968952538921548)
XLA Ops:
  0.6 0.7 broadcast_in_dim.2.weight
  1.4 0.0 copy-start
  1.4 1.6 copy-done
  2.9 0.0 copy-start.1
  2.9 1.6 copy-done.1
  4.5 0.0 copy-start.2
  4.5 0.7 copy-done.2
  5.2 233.4 %mixture.1 = (f32[64,4096]{1,0:T(8,128)S(1)}, f32[2,4096]{1,0:T(2,128)S(1)}) custom-call(f32[4096,128]{1,0:T(8,128)S(1)} %bitcast.10, f32[4096,128]{1,0:T(8,128)S(1)} %bitcast.11, f32[2,128]{1,0:T(2,128)S(1)} %broadcast_in_dim.2.weight, f32[64]{0:T(128)S(1)} %copy-done.2), custom_call_target="tpu_custom_call" | custom-call | tf_op jit(solution)/shard_map/mixture/pallas_call | solution.py:192
  238.6 1.0 copy.10
  239.5 0.6 copy.11
Async XLA Ops:
  1.4 1.6 copy-start
  2.9 1.6 copy-start.1
  4.5 0.7 copy-start.2

commit v2 on v1

v2 whole, which is shorter than its diff:
```python
import functools
import math

import jax
import jax.numpy as jnp
from jax import lax
from jax.experimental import pallas as pl
from jax.experimental.pallas import tpu as pltpu
from jax.sharding import PartitionSpec as P

MESH = pl.DeviceIdType.MESH
LANES = 128
CHUNKS = 8
LAG = 2
GROUP = 16
LOG2E = 1.4426950408889634
NZ, NX, NY = 8, 2, 4


def pair_sum(x, even):
    return x + jnp.where(even, pltpu.roll(x, 7, 0), pltpu.roll(x, 1, 0))


def kernel(n_lat, mode, var, weight, offset, dens, mom, relay, buf, wbuf, wnorm, coef, sem1, sem2, wsem):
    c = lax.axis_index("cfg")
    l = lax.axis_index("lat")
    z, xl, y = c // (NX * NY), (c // NY) % NX, c % NY
    row = xl * n_lat + l
    n_row = NX * n_lat
    plane = z * NY + y
    n_plane = NZ * NY
    n_cfg = NZ * NX * NY
    size = buf.shape[3]

    def remote(src, dst, send, recv, device):
        return pltpu.make_async_remote_copy(
            src_ref=src, dst_ref=dst, send_sem=send, recv_sem=recv, device_id=device, device_id_type=MESH)

    def first_hop(j):
        def ends(i):
            t = lax.rem(i + row, n_row)
            tx, tl = t // n_lat, lax.rem(t, n_lat)
            rows = pl.ds(j * size, size)
            return tx, tl, [(ref.at[:, tx, :, tl, rows], relay.at[j, l, :, :, xl, a]) for a, ref in enumerate((mode, var))]

        for src, dst in ends(0)[2]:
            pltpu.make_async_copy(src, dst, sem1.at[1, j]).start()

        def body(i, carry):
            tx, tl, pairs = ends(i)
            for src, dst in pairs:
                remote(src, dst, sem1.at[0, j], sem1.at[1, j], (z * NX * NY + tx * NY + y, tl)).start()
            return carry

        lax.fori_loop(1, n_row, body, 0)

    def second_hop(j):
        pltpu.make_async_copy(relay.at[j], relay.at[j], sem1.at[1, j]).wait()
        mine = pl.ds(plane * NX, NX)

        def body(i, carry):
            tz = lax.rem(z + 3 * i, NZ)
            ty = lax.rem(y + i // NZ, NY)
            remote(relay.at[j, tz // 2, lax.rem(tz, 2), ty], buf.at[j, mine], sem2.at[0, j], sem2.at[1, j],
                   (tz * NX * NY + xl * NY + ty, l)).start()
            return carry

        lax.fori_loop(1, n_plane, body, 0)
        buf[j, mine] = relay[j, z // 2, lax.rem(z, 2), y]

    def send_weights(i, carry):
        d = lax.rem(i + c, n_cfg)
        tc, tl = l * (n_cfg // n_lat) + d // n_lat, lax.rem(d, n_lat)
        own = jnp.logical_and(tc == c, tl == l)
        slot = wbuf.at[plane * NX + xl]

        @pl.when(own)
        def _():
            slot[...] = weight[...]

        @pl.when(jnp.logical_not(own))
        def _():
            remote(weight, slot, wsem.at[0], wsem.at[1], (tc, tl)).start()

        return carry

    for j in range(CHUNKS):
        first_hop(j)
    lax.fori_loop(0, n_cfg, send_weights, 0)

    parity = lax.broadcasted_iota(jnp.int32, (8, LANES), 0)
    even = lax.rem(parity, 2) == 0
    zero = jnp.zeros((8, LANES), jnp.float32)
    receives_own = z // 2 == l

    def normalize_weights():
        @pl.when(receives_own)
        def _():
            pltpu.make_async_copy(wbuf.at[pl.ds(0, n_cfg - 1)], wbuf.at[pl.ds(0, n_cfg - 1)], wsem.at[1]).wait()

        @pl.when(jnp.logical_not(receives_own))
        def _():
            pltpu.make_async_copy(wbuf, wbuf, wsem.at[1]).wait()

        def spread_weight(s, total):
            w = jnp.where(even, jnp.broadcast_to(wbuf[s, 0:1, :], (8, LANES)), jnp.broadcast_to(wbuf[s, 1:2, :], (8, LANES)))
            wnorm[s] = w
            return total + w

        total = pair_sum(lax.fori_loop(0, n_cfg, spread_weight, zero, unroll=8), even)

        def divide_weight(s, carry):
            wnorm[s] = wnorm[s] / total
            return carry

        lax.fori_loop(0, n_cfg, divide_weight, 0, unroll=8)

    def evaluate(j):
        pltpu.make_async_copy(buf.at[j, pl.ds(0, n_cfg - NX)], buf.at[j, pl.ds(0, n_cfg - NX)], sem2.at[1, j]).wait()

        def tile(q, carry):
            at = pl.ds(pl.multiple_of(q * 8, 8), 8)

            def first_moment(s, acc):
                return acc + wnorm[s] * buf[j, s, 0, at, :]

            centre = pair_sum(lax.fori_loop(0, n_cfg, first_moment, zero, unroll=8), even)

            def second_moment(s, acc):
                dev = buf[j, s, 0, at, :] - centre
                return acc + wnorm[s] * (buf[j, s, 1, at, :] + dev * dev)

            spread = jnp.sqrt(pair_sum(lax.fori_loop(0, n_cfg, second_moment, zero, unroll=8), even))

            def prepare(s, carry):
                root = lax.rsqrt(buf[j, s, 1, at, :])
                scale = root * math.sqrt(0.5 * LOG2E)
                coef[0, s] = scale * (centre - buf[j, s, 0, at, :])
                coef[1, s] = scale * spread
                coef[2, s] = wnorm[s] * root * (1.0 / math.sqrt(2.0 * math.pi))
                return carry

            lax.fori_loop(0, n_cfg, prepare, 0, unroll=8)

            column = (j * size + q * 8) * (LANES // 2)
            for t in range(4):
                lanes = pl.ds(pl.multiple_of(column + t * LANES, LANES), LANES)
                mom[0:1, lanes] = centre[2 * t : 2 * t + 1, :]
                mom[1:2, lanes] = spread[2 * t : 2 * t + 1, :]

            for base in range(0, dens.shape[0], GROUP):
                grid = [jnp.full((8, LANES), offset[base + g], jnp.float32) for g in range(GROUP)]

                def add_source(s, accs):
                    a, b, k = coef[0, s], coef[1, s], coef[2, s]
                    out = []
                    for g in range(GROUP):
                        x = a + grid[g] * b
                        out.append(accs[g] + k * jnp.exp2(-(x * x)))
                    return tuple(out)

                accs = lax.fori_loop(0, n_cfg, add_source, (zero,) * GROUP, unroll=2)
                for g in range(GROUP):
                    value = spread * pair_sum(accs[g], even)
                    for t in range(4):
                        lanes = pl.ds(pl.multiple_of(column + t * LANES, LANES), LANES)
                        dens[base + g : base + g + 1, lanes] = value[2 * t : 2 * t + 1, :]
            return carry

        lax.fori_loop(0, size // 8, tile, 0)

    def evaluate_step(j, carry):
        evaluate(j)
        return carry

    for j in range(CHUNKS):
        second_hop(j)
        if j == LAG - 1:
            normalize_weights()
        if j >= LAG:
            lax.fori_loop(j - LAG, j - LAG + 1, evaluate_step, 0)
    lax.fori_loop(CHUNKS - LAG, CHUNKS, evaluate_step, 0)

    def finish_first(i, carry):
        for j in range(CHUNKS):
            for a in range(2):
                pltpu.make_async_copy(relay.at[j, 0, :, :, 0, a], relay.at[j, 0, :, :, 0, a], sem1.at[0, j]).wait()
        return carry

    lax.fori_loop(1, n_row, finish_first, 0)
    for j in range(CHUNKS):
        pltpu.make_async_copy(buf.at[j, pl.ds(0, n_cfg - NX)], buf.at[j, pl.ds(0, n_cfg - NX)], sem2.at[0, j]).wait()

    @pl.when(receives_own)
    def _():
        pltpu.make_async_copy(wbuf.at[pl.ds(0, n_cfg - 1)], wbuf.at[pl.ds(0, n_cfg - 1)], wsem.at[0]).wait()

    @pl.when(jnp.logical_not(receives_own))
    def _():
        pltpu.make_async_copy(wbuf, wbuf, wsem.at[0]).wait()


def per_device(latent_mode, latent_var, config_weight, grid_offset):
    n_cfg = lax.axis_size("cfg")
    n_lat = lax.axis_size("lat")
    own, width = latent_mode.shape
    grid = grid_offset.shape[0]
    lat_dev = width // n_cfg
    block = own * lat_dev // LANES
    size = block // CHUNKS

    def rows(a):
        a = a.reshape(own, width // LANES, LANES).transpose(1, 0, 2)
        return a.reshape(n_cfg // n_lat // (NX * NY), NX, NY, n_lat, block, LANES)

    weight = jnp.broadcast_to(config_weight[:, None], (own, LANES))
    vmem = pl.BlockSpec(memory_space=pltpu.VMEM)
    hbm = pl.BlockSpec(memory_space=pl.ANY)
    return pl.pallas_call(
        functools.partial(kernel, n_lat),
        out_shape=(
            jax.ShapeDtypeStruct((grid, lat_dev), jnp.float32),
            jax.ShapeDtypeStruct((2, lat_dev), jnp.float32),
        ),
        in_specs=[hbm, hbm, vmem, pl.BlockSpec(memory_space=pltpu.SMEM)],
        out_specs=(vmem, vmem),
        scratch_shapes=[
            pltpu.VMEM((CHUNKS, n_lat, NZ // n_lat, NY, NX, 2, size, LANES), jnp.float32),
            pltpu.VMEM((CHUNKS, n_cfg, 2, size, LANES), jnp.float32),
            pltpu.VMEM((n_cfg, own, LANES), jnp.float32),
            pltpu.VMEM((n_cfg, 8, LANES), jnp.float32),
            pltpu.VMEM((3, n_cfg, 8, LANES), jnp.float32),
            pltpu.SemaphoreType.DMA((2, CHUNKS)),
            pltpu.SemaphoreType.DMA((2, CHUNKS)),
            pltpu.SemaphoreType.DMA((2,)),
        ],
        compiler_params=pltpu.CompilerParams(has_side_effects=True, vmem_limit_bytes=61 * 1024 * 1024),
        name="mixture",
    )(rows(latent_mode), rows(latent_var), weight, grid_offset)


def solution(mesh):
    return jax.shard_map(
        per_device,
        mesh=mesh,
        in_specs=(P("cfg", "lat"), P("cfg", "lat"), P("cfg"), P()),
        out_specs=(P(None, ("cfg", "lat")), P(None, ("cfg", "lat"))),
        check_vma=False,
    )
```

time: 240 us -> 153 us (0.64)
  the two profiles are of different devices: /device:TPU:195 before, /device:TPU:1 now
where the time goes in v2:
time: 153 us; the launch traced here: 152 us
  Pallas kernels  148 us (97%)
  local copies, waits for them, and re-layouts  4.18 us (3%)
    pallas_call x1, Pallas kernels, per_device(): pl.pallas_call(functools.partial(kernel, n_lat), out_shape=(jax.ShapeDtyp...  148 us

profile of v2, /device:TPU:1, one launch (start us, length us, event | category | flops | bytes accessed | tf_op | source)
XLA Modules:
  0.0 152.4 jit_solution(12969585771017298891)
XLA Ops:
  0.6 1.3 broadcast_in_dim.2.weight
  1.9 147.6 %mixture.1 = (f32[64,4096]{1,0:T(8,128)}, f32[2,4096]{1,0:T(2,128)}) custom-call(f32[2,2,4,4,64,128]{5,4,3,2,1,0:T(8,128)} %bitcast.10, f32[2,2,4,4,64,128]{5,4,3,2,1,0:T(8,128)} %bitcast.11, f32[2,128]{1,0:T(2,128)} %broadcast_in_dim.2.weight, f32[64]{0:T(128)} %offset.1), custom_call_target="tpu_custom_call" | custom-call | tf_op jit(solution)/shard_map/mixture/pallas_call | solution.py:219
  149.5 0.0 copy-start
  149.5 2.3 %copy.10 = f32[64,4096]{1,0:T(8,128)} copy(f32[64,4096]{1,0:T(8,128)} %get-tuple-element.4) | data formatting | bytes 2097152
  151.8 0.0 copy-done
  151.8 0.6 copy.11
Async XLA Ops:
  149.5 2.3 %copy-start = (f32[2,4096]{1,0:T(2,128)S(1)}, f32[2,4096]{1,0:T(2,128)}, u32[]{:S(2)}) copy-start(f32[2,4096]{1,0:T(2,128)} %get-tuple-element.5) | copy-start | bytes 98308

commit v3 on v2

--- a/solution.py
+++ b/solution.py
@@ -12,6 +12,7 @@
 LANES = 128
 CHUNKS = 8
 LAG = 2
+AHEAD = 1
 GROUP = 16
 LOG2E = 1.4426950408889634
 NZ, NX, NY = 8, 2, 4
@@ -21,7 +22,7 @@
     return x + jnp.where(even, pltpu.roll(x, 7, 0), pltpu.roll(x, 1, 0))
 
 
-def kernel(n_lat, mode, var, weight, offset, dens, mom, relay, buf, wbuf, wnorm, coef, sem1, sem2, wsem):
+def kernel(n_lat, mode, var, weight, offset, dens, mom, relay, buf, wpair, wbuf, wnorm, coef, sem1, sem2, wsem):
     c = lax.axis_index("cfg")
     l = lax.axis_index("lat")
     z, xl, y = c // (NX * NY), (c // NY) % NX, c % NY
@@ -36,71 +37,93 @@
         return pltpu.make_async_remote_copy(
             src_ref=src, dst_ref=dst, send_sem=send, recv_sem=recv, device_id=device, device_id_type=MESH)
 
-    def first_hop(j):
-        def ends(i):
-            t = lax.rem(i + row, n_row)
-            tx, tl = t // n_lat, lax.rem(t, n_lat)
-            rows = pl.ds(j * size, size)
-            return tx, tl, [(ref.at[:, tx, :, tl, rows], relay.at[j, l, :, :, xl, a]) for a, ref in enumerate((mode, var))]
-
-        for src, dst in ends(0)[2]:
-            pltpu.make_async_copy(src, dst, sem1.at[1, j]).start()
+    def first_hop_own(j):
+        rows = pl.ds(j * size, size)
+        for a, ref in enumerate((mode, var)):
+            pltpu.make_async_copy(ref.at[:, xl, :, l, rows], relay.at[j, l, :, :, xl, a], sem1.at[1, j]).start()
+
+    def first_hop_send(j, i):
+        t = lax.rem(i + row, n_row)
+        tx, tl = t // n_lat, lax.rem(t, n_lat)
+        rows = pl.ds(j * size, size)
+        for a, ref in enumerate((mode, var)):
+            remote(ref.at[:, tx, :, tl, rows], relay.at[j, l, :, :, xl, a], sem1.at[0, j], sem1.at[1, j],
+                   (z * NX * NY + tx * NY + y, tl)).start()
+
+    def plane_peer(i):
+        tz = lax.rem(z + 3 * i, NZ)
+        ty = lax.rem(y + i // NZ, NY)
+        return tz, ty, (tz * NX * NY + xl * NY + ty, l)
+
+    mine = pl.ds(plane * NX, NX)
+
+    def second_hop_send(j, i):
+        tz, ty, device = plane_peer(i)
+        remote(relay.at[j, tz // 2, lax.rem(tz, 2), ty], buf.at[j, mine], sem2.at[0, j], sem2.at[1, j], device).start()
+
+    def second_hop(j):
+        if j + AHEAD < CHUNKS:
+            first_hop_own(j + AHEAD)
+        pltpu.make_async_copy(relay.at[j], relay.at[j], sem1.at[1, j]).wait()
+        share = (n_plane - 1) // (n_row - 1)
 
         def body(i, carry):
-            tx, tl, pairs = ends(i)
-            for src, dst in pairs:
-                remote(src, dst, sem1.at[0, j], sem1.at[1, j], (z * NX * NY + tx * NY + y, tl)).start()
-            return carry
-
-        lax.fori_loop(1, n_row, body, 0)
-
-    def second_hop(j):
-        pltpu.make_async_copy(relay.at[j], relay.at[j], sem1.at[1, j]).wait()
-        mine = pl.ds(plane * NX, NX)
+            if j + AHEAD < CHUNKS:
+                first_hop_send(j + AHEAD, i + 1)
+            for k in range(share):
+                second_hop_send(j, i * share + k + 1)
+            return carry
+
+        lax.fori_loop(0, n_row - 1, body, 0)
+        for i in range((n_row - 1) * share + 1, n_plane):
+            second_hop_send(j, i)
+        buf[j, mine] = relay[j, z // 2, lax.rem(z, 2), y]
+
+    for r in range(2):
+        wpair[xl, r : r + 1, :] = jnp.full((1, LANES), weight[r], jnp.float32)
+
+    barrier = pltpu.get_barrier_semaphore()
+
+    def greet_row(i, carry):
+        t = lax.rem(i + row, n_row)
+        pl.semaphore_signal(barrier, inc=1, device_id=(z * NX * NY + (t // n_lat) * NY + y, lax.rem(t, n_lat)), device_id_type=MESH)
+        return carry
+
+    def greet_plane(i, carry):
+        pl.semaphore_signal(barrier, inc=1, device_id=plane_peer(i)[2], device_id_type=MESH)
+        return carry
+
+    lax.fori_loop(1, n_plane, greet_plane, 0)
+    lax.fori_loop(1, n_row, greet_row, 0)
+    pl.semaphore_wait(barrier, n_plane + n_row - 2)
+
+    pair_copy = remote(wpair.at[xl], wpair.at[xl], wsem.at[0], wsem.at[1], (z * NX * NY + (1 - xl) * NY + y, l))
+    pair_copy.start()
+    for j in range(min(AHEAD, CHUNKS)):
+        first_hop_own(j)
+
+        def start_row(i, carry):
+            first_hop_send(j, i)
+            return carry
+
+        lax.fori_loop(1, n_row, start_row, 0)
+
+    def send_weights():
+        pair_copy.wait()
 
         def body(i, carry):
-            tz = lax.rem(z + 3 * i, NZ)
-            ty = lax.rem(y + i // NZ, NY)
-            remote(relay.at[j, tz // 2, lax.rem(tz, 2), ty], buf.at[j, mine], sem2.at[0, j], sem2.at[1, j],
-                   (tz * NX * NY + xl * NY + ty, l)).start()
+            remote(wpair, wbuf.at[mine], wsem.at[2], wsem.at[3], plane_peer(i)[2]).start()
             return carry
 
         lax.fori_loop(1, n_plane, body, 0)
-        buf[j, mine] = relay[j, z // 2, lax.rem(z, 2), y]
-
-    def send_weights(i, carry):
-        d = lax.rem(i + c, n_cfg)
-        tc, tl = l * (n_cfg // n_lat) + d // n_lat, lax.rem(d, n_lat)
-        own = jnp.logical_and(tc == c, tl == l)
-        slot = wbuf.at[plane * NX + xl]
-
-        @pl.when(own)
-        def _():
-            slot[...] = weight[...]
-
-        @pl.when(jnp.logical_not(own))
-        def _():
-            remote(weight, slot, wsem.at[0], wsem.at[1], (tc, tl)).start()
-
-        return carry
-
-    for j in range(CHUNKS):
-        first_hop(j)
-    lax.fori_loop(0, n_cfg, send_weights, 0)
+        wbuf[mine] = wpair[...]
 
     parity = lax.broadcasted_iota(jnp.int32, (8, LANES), 0)
     even = lax.rem(parity, 2) == 0
     zero = jnp.zeros((8, LANES), jnp.float32)
-    receives_own = z // 2 == l
 
     def normalize_weights():
-        @pl.when(receives_own)
-        def _():
-            pltpu.make_async_copy(wbuf.at[pl.ds(0, n_cfg - 1)], wbuf.at[pl.ds(0, n_cfg - 1)], wsem.at[1]).wait()
-
-        @pl.when(jnp.logical_not(receives_own))
-        def _():
-            pltpu.make_async_copy(wbuf, wbuf, wsem.at[1]).wait()
+        pltpu.make_async_copy(wbuf.at[pl.ds(0, n_cfg - NX)], wbuf.at[pl.ds(0, n_cfg - NX)], wsem.at[3]).wait()
 
         def spread_weight(s, total):
             w = jnp.where(even, jnp.broadcast_to(wbuf[s, 0:1, :], (8, LANES)), jnp.broadcast_to(wbuf[s, 1:2, :], (8, LANES)))
@@ -175,6 +198,8 @@
 
     for j in range(CHUNKS):
         second_hop(j)
+        if j == 0:
+            send_weights()
         if j == LAG - 1:
             normalize_weights()
         if j >= LAG:
@@ -191,13 +216,7 @@
     for j in range(CHUNKS):
         pltpu.make_async_copy(buf.at[j, pl.ds(0, n_cfg - NX)], buf.at[j, pl.ds(0, n_cfg - NX)], sem2.at[0, j]).wait()
 
-    @pl.when(receives_own)
-    def _():
-        pltpu.make_async_copy(wbuf.at[pl.ds(0, n_cfg - 1)], wbuf.at[pl.ds(0, n_cfg - 1)], wsem.at[0]).wait()
-
-    @pl.when(jnp.logical_not(receives_own))
-    def _():
-        pltpu.make_async_copy(wbuf, wbuf, wsem.at[0]).wait()
+    pltpu.make_async_copy(wbuf.at[pl.ds(0, n_cfg - NX)], wbuf.at[pl.ds(0, n_cfg - NX)], wsem.at[2]).wait()
 
 
 def per_device(latent_mode, latent_var, config_weight, grid_offset):
@@ -213,8 +232,8 @@
         a = a.reshape(own, width // LANES, LANES).transpose(1, 0, 2)
         return a.reshape(n_cfg // n_lat // (NX * NY), NX, NY, n_lat, block, LANES)
 
-    weight = jnp.broadcast_to(config_weight[:, None], (own, LANES))
     vmem = pl.BlockSpec(memory_space=pltpu.VMEM)
+    smem = pl.BlockSpec(memory_space=pltpu.SMEM)
     hbm = pl.BlockSpec(memory_space=pl.ANY)
     return pl.pallas_call(
         functools.partial(kernel, n_lat),
@@ -222,21 +241,22 @@
             jax.ShapeDtypeStruct((grid, lat_dev), jnp.float32),
             jax.ShapeDtypeStruct((2, lat_dev), jnp.float32),
         ),
-        in_specs=[hbm, hbm, vmem, pl.BlockSpec(memory_space=pltpu.SMEM)],
+        in_specs=[hbm, hbm, smem, smem],
         out_specs=(vmem, vmem),
         scratch_shapes=[
             pltpu.VMEM((CHUNKS, n_lat, NZ // n_lat, NY, NX, 2, size, LANES), jnp.float32),
             pltpu.VMEM((CHUNKS, n_cfg, 2, size, LANES), jnp.float32),
+            pltpu.VMEM((NX, own, LANES), jnp.float32),
             pltpu.VMEM((n_cfg, own, LANES), jnp.float32),
             pltpu.VMEM((n_cfg, 8, LANES), jnp.float32),
             pltpu.VMEM((3, n_cfg, 8, LANES), jnp.float32),
             pltpu.SemaphoreType.DMA((2, CHUNKS)),
             pltpu.SemaphoreType.DMA((2, CHUNKS)),
-            pltpu.SemaphoreType.DMA((2,)),
+            pltpu.SemaphoreType.DMA((4,)),
         ],
-        compiler_params=pltpu.CompilerParams(has_side_effects=True, vmem_limit_bytes=61 * 1024 * 1024),
+        compiler_params=pltpu.CompilerParams(collective_id=0, has_side_effects=True, vmem_limit_bytes=61 * 1024 * 1024),
         name="mixture",
-    )(rows(latent_mode), rows(latent_var), weight, grid_offset)
+    )(rows(latent_mode), rows(latent_var), config_weight, grid_offset)
 
 
 def solution(mesh):

time: 153 us -> 125 us (0.82)
  Pallas kernels: 148 us -> 122 us
    pallas_call x1, Pallas kernels: 148 us -> 122 us  [per_device(): pl.pallas_call(functools.partial(kernel, n_lat), out_shape=(jax.ShapeDtyp...]
where the time goes in v3:
time: 125 us
  Pallas kernels  122 us (98%)
  local copies, waits for them, and re-layouts  2.89 us (2%)
    pallas_call x1, Pallas kernels, per_device(): pl.pallas_call(functools.partial(kernel, n_lat), out_shape=(jax.ShapeDtyp...  122 us
    unnamed x4, local copies, waits for them, and re-layouts  2.89 us

profile of v3, /device:TPU:1, one launch (start us, length us, event | category | flops | bytes accessed | tf_op | source)
XLA Modules:
  0.0 125.3 jit_solution(18067299775514413265)
XLA Ops:
  0.6 121.8 %mixture.1 = (f32[64,4096]{1,0:T(8,128)}, f32[2,4096]{1,0:T(2,128)}) custom-call(f32[2,2,4,4,64,128]{5,4,3,2,1,0:T(8,128)} %bitcast.10, f32[2,2,4,4,64,128]{5,4,3,2,1,0:T(8,128)} %bitcast.11, f32[2]{0:T(128)} %weight.1, f32[64]{0:T(128)} %offset.1), custom_call_target="tpu_custom_call" | custom-call | tf_op jit(solution)/shard_map/mixture/pallas_call | solution.py:238
  122.4 0.0 copy-start
  122.4 2.3 %copy.10 = f32[64,4096]{1,0:T(8,128)} copy(f32[64,4096]{1,0:T(8,128)} %get-tuple-element.4) | data formatting | bytes 2097152
  124.7 0.0 copy-done
  124.7 0.6 copy.11
Async XLA Ops:
  122.4 2.3 %copy-start = (f32[2,4096]{1,0:T(2,128)S(1)}, f32[2,4096]{1,0:T(2,128)}, u32[]{:S(2)}) copy-start(f32[2,4096]{1,0:T(2,128)} %get-tuple-element.5) | copy-start | bytes 98308

commit v4 on v3

--- a/solution.py
+++ b/solution.py
@@ -12,21 +12,22 @@
 LANES = 128
 CHUNKS = 8
 LAG = 2
-AHEAD = 1
+AHEAD = 2
 GROUP = 16
 LOG2E = 1.4426950408889634
 NZ, NX, NY = 8, 2, 4
+LAT_ORDER = (0, 2, 1, 3)
+ROW_ORDER = ((1, 0), (0, 2), (1, 2), (0, 1), (1, 1), (0, 3), (1, 3))
 
 
 def pair_sum(x, even):
     return x + jnp.where(even, pltpu.roll(x, 7, 0), pltpu.roll(x, 1, 0))
 
 
-def kernel(n_lat, mode, var, weight, offset, dens, mom, relay, buf, wpair, wbuf, wnorm, coef, sem1, sem2, wsem):
+def kernel(n_lat, mode, var, weight, offset, dens, mom, relay, buf, wpair, wbuf, wnorm, coef, sem1, sem1r, sem2, wsem):
     c = lax.axis_index("cfg")
     l = lax.axis_index("lat")
     z, xl, y = c // (NX * NY), (c // NY) % NX, c % NY
-    row = xl * n_lat + l
     n_row = NX * n_lat
     plane = z * NY + y
     n_plane = NZ * NY
@@ -40,15 +41,19 @@
     def first_hop_own(j):
         rows = pl.ds(j * size, size)
         for a, ref in enumerate((mode, var)):
-            pltpu.make_async_copy(ref.at[:, xl, :, l, rows], relay.at[j, l, :, :, xl, a], sem1.at[1, j]).start()
-
-    def first_hop_send(j, i):
-        t = lax.rem(i + row, n_row)
-        tx, tl = t // n_lat, lax.rem(t, n_lat)
+            pltpu.make_async_copy(ref.at[:, xl, :, l, rows], relay.at[j, l, :, :, xl, a], sem1r.at[j, l]).start()
+
+    def first_hop_send(j, tx, tl):
         rows = pl.ds(j * size, size)
         for a, ref in enumerate((mode, var)):
-            remote(ref.at[:, tx, :, tl, rows], relay.at[j, l, :, :, xl, a], sem1.at[0, j], sem1.at[1, j],
+            remote(ref.at[:, tx, :, tl, rows], relay.at[j, l, :, :, xl, a], sem1.at[j], sem1r.at[j, l],
                    (z * NX * NY + tx * NY + y, tl)).start()
+
+    def row_peer(i):
+        return (xl + ROW_ORDER[i][0]) % NX, lax.rem(l + ROW_ORDER[i][1], n_lat)
+
+    def first_hop_wait(j, source):
+        pltpu.make_async_copy(relay.at[j, source], relay.at[j, source], sem1r.at[j, source]).wait()
 
     def plane_peer(i):
         tz = lax.rem(z + 3 * i, NZ)
@@ -57,56 +62,69 @@
 
     mine = pl.ds(plane * NX, NX)
 
-    def second_hop_send(j, i):
-        tz, ty, device = plane_peer(i)
-        remote(relay.at[j, tz // 2, lax.rem(tz, 2), ty], buf.at[j, mine], sem2.at[0, j], sem2.at[1, j], device).start()
-
-    def second_hop(j):
-        if j + AHEAD < CHUNKS:
-            first_hop_own(j + AHEAD)
-        pltpu.make_async_copy(relay.at[j], relay.at[j], sem1.at[1, j]).wait()
+    def second_hop_send(j, tz, ty):
+        remote(relay.at[j, tz // 2, lax.rem(tz, 2), ty], buf.at[j, mine], sem2.at[0, j], sem2.at[1, j],
+               (tz * NX * NY + xl * NY + ty, l)).start()
+
+    def second_hop_opening(following):
+        pairs = [(j, i) for j in following for i in range(n_row - 1)]
+        for j in following:
+            first_hop_own(j)
+        for step, turn in enumerate(LAT_ORDER):
+            source = lax.rem(l + n_lat - turn, n_lat)
+            first_hop_wait(0, source)
+            share = pairs[step * len(pairs) // n_lat : (step + 1) * len(pairs) // n_lat]
+            for i in range(2 * NY):
+                if i % 2 == 0 and i // 2 < len(share):
+                    j, peer = share[i // 2]
+                    first_hop_send(j, *row_peer(peer))
+                tz, ty = 2 * source + i % 2, lax.rem(y + i // 2, NY)
+                if i // 2 > 0:
+                    second_hop_send(0, tz, ty)
+                else:
+                    @pl.when(tz != z)
+                    def _():
+                        second_hop_send(0, tz, ty)
+        buf[0, mine] = relay[0, z // 2, lax.rem(z, 2), y]
+
+    def second_hop(j, following):
+        for f in following:
+            first_hop_own(f)
+        for source in range(n_lat):
+            first_hop_wait(j, source)
         share = (n_plane - 1) // (n_row - 1)
-
-        def body(i, carry):
-            if j + AHEAD < CHUNKS:
-                first_hop_send(j + AHEAD, i + 1)
-            for k in range(share):
-                second_hop_send(j, i * share + k + 1)
-            return carry
-
-        lax.fori_loop(0, n_row - 1, body, 0)
-        for i in range((n_row - 1) * share + 1, n_plane):
-            second_hop_send(j, i)
+        for i in range(n_row - 1):
+            for f in following:
+                first_hop_send(f, *row_peer(i))
+
+            def body(k, carry):
+                tz, ty, _ = plane_peer(k)
+                second_hop_send(j, tz, ty)
+                return carry
+
+            lax.fori_loop(i * share + 1, n_plane if i == n_row - 2 else (i + 1) * share + 1, body, 0)
         buf[j, mine] = relay[j, z // 2, lax.rem(z, 2), y]
 
     for r in range(2):
         wpair[xl, r : r + 1, :] = jnp.full((1, LANES), weight[r], jnp.float32)
 
     barrier = pltpu.get_barrier_semaphore()
-
-    def greet_row(i, carry):
-        t = lax.rem(i + row, n_row)
-        pl.semaphore_signal(barrier, inc=1, device_id=(z * NX * NY + (t // n_lat) * NY + y, lax.rem(t, n_lat)), device_id_type=MESH)
-        return carry
 
     def greet_plane(i, carry):
         pl.semaphore_signal(barrier, inc=1, device_id=plane_peer(i)[2], device_id_type=MESH)
         return carry
 
     lax.fori_loop(1, n_plane, greet_plane, 0)
-    lax.fori_loop(1, n_row, greet_row, 0)
+    for i in range(n_row - 1):
+        tx, tl = row_peer(i)
+        pl.semaphore_signal(barrier, inc=1, device_id=(z * NX * NY + tx * NY + y, tl), device_id_type=MESH)
+    first_hop_own(0)
     pl.semaphore_wait(barrier, n_plane + n_row - 2)
 
+    for i in range(n_row - 1):
+        first_hop_send(0, *row_peer(i))
     pair_copy = remote(wpair.at[xl], wpair.at[xl], wsem.at[0], wsem.at[1], (z * NX * NY + (1 - xl) * NY + y, l))
     pair_copy.start()
-    for j in range(min(AHEAD, CHUNKS)):
-        first_hop_own(j)
-
-        def start_row(i, carry):
-            first_hop_send(j, i)
-            return carry
-
-        lax.fori_loop(1, n_row, start_row, 0)
 
     def send_weights():
         pair_copy.wait()
@@ -197,7 +215,10 @@
         return carry
 
     for j in range(CHUNKS):
-        second_hop(j)
+        if j == 0:
+            second_hop_opening(range(1, min(AHEAD, CHUNKS - 1) + 1))
+        else:
+            second_hop(j, [j + AHEAD] if j + AHEAD < CHUNKS else [])
         if j == 0:
             send_weights()
         if j == LAG - 1:
@@ -209,7 +230,7 @@
     def finish_first(i, carry):
         for j in range(CHUNKS):
             for a in range(2):
-                pltpu.make_async_copy(relay.at[j, 0, :, :, 0, a], relay.at[j, 0, :, :, 0, a], sem1.at[0, j]).wait()
+                pltpu.make_async_copy(relay.at[j, 0, :, :, 0, a], relay.at[j, 0, :, :, 0, a], sem1.at[j]).wait()
         return carry
 
     lax.fori_loop(1, n_row, finish_first, 0)
@@ -234,7 +255,7 @@
 
     vmem = pl.BlockSpec(memory_space=pltpu.VMEM)
     smem = pl.BlockSpec(memory_space=pltpu.SMEM)
-    hbm = pl.BlockSpec(memory_space=pl.ANY)
+    hbm = pl.BlockSpec(memory_space=pltpu.HBM)
     return pl.pallas_call(
         functools.partial(kernel, n_lat),
         out_shape=(
@@ -250,11 +271,12 @@
             pltpu.VMEM((n_cfg, own, LANES), jnp.float32),
             pltpu.VMEM((n_cfg, 8, LANES), jnp.float32),
             pltpu.VMEM((3, n_cfg, 8, LANES), jnp.float32),
-            pltpu.SemaphoreType.DMA((2, CHUNKS)),
+            pltpu.SemaphoreType.DMA((CHUNKS,)),
+            pltpu.SemaphoreType.DMA((CHUNKS, n_lat)),
             pltpu.SemaphoreType.DMA((2, CHUNKS)),
             pltpu.SemaphoreType.DMA((4,)),
         ],
-        compiler_params=pltpu.CompilerParams(collective_id=0, has_side_effects=True, vmem_limit_bytes=61 * 1024 * 1024),
+        compiler_params=pltpu.CompilerParams(collective_id=0, has_side_effects=True, vmem_limit_bytes=52 * 1024 * 1024),
         name="mixture",
     )(rows(latent_mode), rows(latent_var), config_weight, grid_offset)
 

time: 125 us -> 119 us (0.952)
  Pallas kernels: 122 us -> 116 us
    pallas_call x1, Pallas kernels: 122 us -> 116 us  [per_device(): pl.pallas_call(functools.partial(kernel, n_lat), out_shape=(jax.ShapeDtyp...]
    unnamed x4 -> x6, local copies, waits for them, and re-layouts: 2.89 us -> 2.89 us
where the time goes in v4:
time: 119 us
  Pallas kernels  116 us (97%)
  local copies, waits for them, and re-layouts  2.89 us (2%)
    pallas_call x1, Pallas kernels, per_device(): pl.pallas_call(functools.partial(kernel, n_lat), out_shape=(jax.ShapeDtyp...  116 us
    unnamed x6, local copies, waits for them, and re-layouts  2.89 us

profile of v4, /device:TPU:1, one launch (start us, length us, event | category | flops | bytes accessed | tf_op | source)
XLA Modules:
  0.0 119.2 jit_solution(14515505524167776042)
XLA Ops:
  0.6 0.0 copy-start
  0.6 0.6 copy-done
  1.3 0.0 copy-start.1
  1.3 0.7 copy-done.1
  1.9 115.7 %mixture.1 = (f32[64,4096]{1,0:T(8,128)S(1)}, f32[2,4096]{1,0:T(2,128)S(1)}) custom-call(f32[2,2,4,4,64,128]{5,4,3,2,1,0:T(8,128)} %bitcast.10, f32[2,2,4,4,64,128]{5,4,3,2,1,0:T(8,128)} %bitcast.11, f32[2]{0:T(128)S(1)} %copy-done, f32[64]{0:T(128)S(1)} %copy-done.1), custom_call_target="tpu_custom_call" | custom-call | tf_op jit(solution)/shard_map/mixture/pallas_call | solution.py:259
  117.6 1.0 copy.10
  118.6 0.6 copy.11
Async XLA Ops:
  0.6 0.7 copy-start
  1.3 0.7 copy-start.1

commit v5 on v4

v5 whole, which is shorter than its diff:
```python
import functools
import math

import jax
import jax.numpy as jnp
from jax import lax
from jax.experimental import pallas as pl
from jax.experimental.pallas import tpu as pltpu
from jax.sharding import PartitionSpec as P

MESH = pl.DeviceIdType.MESH
LANES = 128
CHUNKS = 8
LAG = 2
AHEAD = 2
GROUP = 16
UNROLL = 4
MERGED = 5
DIST_ORDER = (4, 2, 6, 3, 5, 1, 7, 0)
LOG2E = 1.4426950408889634
NZ, NX, NY = 8, 2, 4
LAT_ORDER = (0, 2, 1, 3)
ROW_ORDER = ((1, 0), (0, 2), (1, 2), (0, 1), (1, 1), (0, 3), (1, 3))


def pair_sum(x, even):
    return x + jnp.where(even, pltpu.roll(x, 7, 0), pltpu.roll(x, 1, 0))


def kernel(n_lat, mode, var, weight, offset, dens, mom, relay, buf, wpair, wbuf, wnorm, wslot, coef, share_w, stat_own, stat_out, stat_in,
           line_own, line_out, line_in, part_out, part_in, sem1, sem1r, sem2, wsem, sem3):
    c = lax.axis_index("cfg")
    l = lax.axis_index("lat")
    z, xl, y = c // (NX * NY), (c // NY) % NX, c % NY
    n_row = NX * n_lat
    plane = z * NY + y
    n_plane = NZ * NY
    n_cfg = NZ * NX * NY
    size = buf.shape[3]

    def remote(src, dst, send, recv, device):
        return pltpu.make_async_remote_copy(
            src_ref=src, dst_ref=dst, send_sem=send, recv_sem=recv, device_id=device, device_id_type=MESH)

    def first_hop_own(j):
        rows = pl.ds(j * size, size)
        for a, ref in enumerate((mode, var)):
            pltpu.make_async_copy(ref.at[:, xl, :, l, rows], relay.at[j, l, :, :, xl, a], sem1r.at[j, l]).start()

    def first_hop_send(j, tx, tl):
        rows = pl.ds(j * size, size)
        for a, ref in enumerate((mode, var)):
            remote(ref.at[:, tx, :, tl, rows], relay.at[j, l, :, :, xl, a], sem1.at[j], sem1r.at[j, l],
                   (z * NX * NY + tx * NY + y, tl)).start()

    def row_peer(i):
        return (xl + ROW_ORDER[i][0]) % NX, lax.rem(l + ROW_ORDER[i][1], n_lat)

    def first_hop_wait(j, source):
        pltpu.make_async_copy(relay.at[j, source], relay.at[j, source], sem1r.at[j, source]).wait()

    def plane_peer(i):
        tz = lax.rem(z + 3 * i, NZ)
        ty = lax.rem(y + i // NZ, NY)
        return tz, ty, (tz * NX * NY + xl * NY + ty, l)

    mine = pl.ds(plane * NX, NX)

    def block(j, tz, ty):
        return relay.at[j, tz // 2, lax.rem(tz, 2), ty]

    def second_hop_send(j, tz, ty):
        if j >= MERGED:
            remote(block(j, tz, ty), buf.at[j, mine], sem2.at[0, j], sem2.at[1, j], (tz * NX * NY + xl * NY + ty, l)).start()

    odd = lax.rem(y, 2)

    def merge_route(d, dy):
        if d == 0:
            return z, y
        if d < 4:
            return lax.rem(z + NZ - d + 1, NZ), NY * d + y
        if d > 4:
            return lax.rem(z + NZ - d - 1, NZ), NY + 14 + NY * (NZ - d - 1) + y
        return lax.rem(z + 5 + 6 * (dy % 2), NZ), 16 + 14 * (dy % 2) + y // 2

    def merge_send(j, d, dy):
        to_z, slot = merge_route(d, dy)
        ty = lax.rem(y + dy, NY)
        src, dst = block(j, lax.rem(z + NZ - d, NZ), ty), buf.at[j, pl.ds(slot * NX, NX)]
        if dy == 0 and d in (0, 1, NZ - 1):
            dst[...] = src[...]
        else:
            remote(src, dst, sem2.at[0, j], sem2.at[1, j], (to_z * NX * NY + xl * NY + ty, l)).start()

    def merge_opening(source, half, dy):
        dz = 2 * source + half
        d = lax.rem(z + NZ - dz, NZ)
        up, down = jnp.logical_and(d >= 1, d <= 3), d >= 5
        slot = jnp.where(up, NY * d + y, jnp.where(down, NY + 14 + NY * (NZ - 1 - d) + y, jnp.where(d == 0, y, 16 + 14 * (dy % 2) + y // 2)))
        step = jnp.where(up, 1, jnp.where(down, NZ - 1, jnp.where(d == 0, 0, 1 + (NZ - 2) * (dy % 2))))
        to_z, ty = lax.rem(dz + step, NZ), lax.rem(y + dy, NY)
        src, dst = relay.at[0, source, half, ty], buf.at[0, pl.ds(slot * NX, NX)]

        def send():
            remote(src, dst, sem2.at[0, 0], sem2.at[1, 0], (to_z * NX * NY + xl * NY + ty, l)).start()

        if dy:
            send()
        else:
            pl.when(to_z != z)(send)

    def second_hop(j, following):
        pairs = [(f, i) for f in following for i in range(n_row - 1)]
        for f in following:
            first_hop_own(f)
        if j == 0:
            for step, turn in enumerate(LAT_ORDER):
                source = lax.rem(l + n_lat - turn, n_lat)
                first_hop_wait(0, source)
                for i in range(2 * NY):
                    merge_opening(source, i % 2, (i // 2 + 1) % NY)
                    if i % 2 == 1 and pairs:
                        f, peer = pairs.pop(0)
                        first_hop_send(f, *row_peer(peer))
            for d in (0, 1, NZ - 1):
                merge_send(0, d, 0)
            return
        for source in range(n_lat):
            first_hop_wait(j, source)
        if j < MERGED:
            for n, (dy, d) in enumerate((dy, d) for dy in range(NY) for d in DIST_ORDER):
                if n % 2 == 0 and n // 2 < len(pairs):
                    f, peer = pairs[n // 2]
                    first_hop_send(f, *row_peer(peer))
                merge_send(j, d, dy)
            return
        share = (n_plane - 1) // (n_row - 1)
        for i in range(n_row - 1):
            for f in following:
                first_hop_send(f, *row_peer(i))

            def body(k, carry):
                tz, ty, _ = plane_peer(k)
                second_hop_send(j, tz, ty)
                return carry

            lax.fori_loop(i * share + 1, n_plane if i == n_row - 2 else (i + 1) * share + 1, body, 0)
        buf[j, mine] = block(j, z, y)[...]

    for r in range(2):
        wpair[xl, r : r + 1, :] = jnp.full((1, LANES), weight[r], jnp.float32)

    barrier = pltpu.get_barrier_semaphore()

    def greet_plane(i, carry):
        pl.semaphore_signal(barrier, inc=1, device_id=plane_peer(i)[2], device_id_type=MESH)
        return carry

    lax.fori_loop(1, n_plane, greet_plane, 0)
    for i in range(n_row - 1):
        tx, tl = row_peer(i)
        pl.semaphore_signal(barrier, inc=1, device_id=(z * NX * NY + tx * NY + y, tl), device_id_type=MESH)
    first_hop_own(0)
    pl.semaphore_wait(barrier, n_plane + n_row - 2)

    for i in range(n_row - 1):
        first_hop_send(0, *row_peer(i))
    pair_copy = remote(wpair.at[xl], wpair.at[xl], wsem.at[0], wsem.at[1], (z * NX * NY + (1 - xl) * NY + y, l))
    pair_copy.start()

    def send_weights():
        pair_copy.wait()

        def body(i, carry):
            remote(wpair, wbuf.at[mine], wsem.at[2], wsem.at[3], plane_peer(i)[2]).start()
            return carry

        lax.fori_loop(1, n_plane, body, 0)
        wbuf[mine] = wpair[...]

    parity = lax.broadcasted_iota(jnp.int32, (8, LANES), 0)
    even = lax.rem(parity, 2) == 0
    zero = jnp.zeros((8, LANES), jnp.float32)

    def normalize_weights():
        pltpu.make_async_copy(wbuf.at[pl.ds(0, n_cfg - NX)], wbuf.at[pl.ds(0, n_cfg - NX)], wsem.at[3]).wait()

        def spread_weight(s, total):
            w = jnp.where(even, jnp.broadcast_to(wbuf[s, 0:1, :], (8, LANES)), jnp.broadcast_to(wbuf[s, 1:2, :], (8, LANES)))
            wnorm[s] = w
            return total + w

        total = pair_sum(lax.fori_loop(0, n_cfg, spread_weight, zero, unroll=8), even)

        def divide_weight(s, carry):
            wnorm[s] = wnorm[s] / total
            return carry

        lax.fori_loop(0, n_cfg, divide_weight, 0, unroll=8)

        def put(slot, plane_z, ys, carry=None):
            for i, yy in enumerate(ys):
                for a in range(NX):
                    wslot[(slot + i) * NX + a] = wnorm[(plane_z * NY + yy) * NX + a]

        def shifted(k):
            return lax.rem(z + NZ + k, NZ)

        put(0, z, range(NY))
        for d in range(1, 4):
            put(NY * d, shifted(d - 1), range(NY))
            put(NY + 14 + NY * (d - 1), shifted(1 - d), range(NY))
        put(16, shifted(3), (odd, odd + 2))
        put(30, shifted(-3), (1 - odd, 3 - odd))

        def weight_of(entries):
            acc = zero
            for plane_z, ys in entries:
                for yy in ys:
                    for a in range(NX):
                        acc = acc + wnorm[(plane_z * NY + yy) * NX + a]
            return pair_sum(acc, even)

        share_w[0] = weight_of([(z, range(NY))])
        share_w[1] = weight_of([(shifted(d), range(NY)) for d in range(1, 4)] + [(shifted(4), (odd, odd + 2))])
        share_w[2] = weight_of([(shifted(-d), range(NY)) for d in range(1, 4)] + [(shifted(4), (1 - odd, 3 - odd))])

    own_slots, far_slots = NX * NY, NX * 14

    def moments(j, w_ref, low, count):
        def first(s, acc):
            return acc[0] + w_ref[low + s] * buf[j, low + s, 0], acc[1] + w_ref[low + s]

        total, weight_sum = lax.fori_loop(0, count, first, (zero, zero), unroll=4)
        mean = pair_sum(total, even) / pair_sum(weight_sum, even)

        def second(s, acc):
            dev = buf[j, low + s, 0] - mean
            return acc + w_ref[low + s] * (buf[j, low + s, 1] + dev * dev)

        return mean, pair_sum(lax.fori_loop(0, count, second, zero, unroll=4), even)

    def accumulate(j, w_ref, low, count, unroll, centre, spread, store):
        def prepare(s, carry):
            var_s = buf[j, low + s, 1]
            coef[0, s] = (-0.5 * LOG2E) / var_s
            coef[1, s] = w_ref[low + s] * lax.rsqrt((2.0 * math.pi) * var_s)
            return carry

        lax.fori_loop(0, count, prepare, 0, unroll=4)

        for base in range(0, dens.shape[0], GROUP):
            points = [centre + offset[base + g] * spread for g in range(GROUP)]

            def add_source(s, accs):
                mean, rate, scale = buf[j, low + s, 0], coef[0, s], coef[1, s]
                out = []
                for g in range(GROUP):
                    gap = points[g] - mean
                    out.append(accs[g] + scale * jnp.exp2(gap * rate * gap))
                return tuple(out)

            accs = lax.fori_loop(0, count, add_source, (zero,) * GROUP, unroll=unroll)
            for g in range(GROUP):
                store(base + g, pair_sum(accs[g], even))

    tiles = 4
    width = tiles * LANES

    def put_rows(ref, row, column, value):
        for t in range(tiles):
            ref[row : row + 1, pl.ds(pl.multiple_of(column + t * LANES, LANES), LANES)] = value[2 * t : 2 * t + 1, :]

    def neighbour(side):
        return (lax.rem(z + NZ - 1 + 2 * side, NZ) * NX * NY + xl * NY + y, l)

    def received(ref, sem):
        pltpu.make_async_copy(ref, ref, sem).wait()

    def wait_blocks(j):
        count = n_cfg - NX * (3 if j < MERGED else 1)
        received(buf.at[j, pl.ds(0, count)], sem2.at[1, j])

    def send_stats(j):
        def side_stats(side, carry):
            mean, second = moments(j, wslot, own_slots + side * far_slots, far_slots)
            stat_out[j, side, 0] = mean
            stat_out[j, side, 1] = second
            return carry

        lax.fori_loop(0, 2, side_stats, 0)
        mean, second = moments(j, wslot, 0, own_slots)
        stat_own[j, 0] = mean
        stat_own[j, 1] = second
        for side in range(2):
            remote(stat_out.at[j, side], stat_in.at[j, side], sem3.at[0, j], sem3.at[1, j], neighbour(side)).start()

    def merge_stats(j):
        received(stat_in.at[j], sem3.at[1, j])
        means = [stat_own[j, 0], stat_in[j, 0, 0], stat_in[j, 1, 0]]
        seconds = [stat_own[j, 1], stat_in[j, 0, 1], stat_in[j, 1, 1]]
        shares = [share_w[i] for i in range(3)]
        centre = shares[0] * means[0] + shares[1] * means[1] + shares[2] * means[2]
        second = seconds[0] + seconds[1] + seconds[2]
        for share, mean in zip(shares, means):
            second = second + share * (mean - centre) * (mean - centre)
        spread = jnp.sqrt(second)
        for ref in (line_own.at[j], line_out.at[j]):
            ref[0] = centre
            ref[1] = spread
        put_rows(mom, 0, j * width, centre)
        put_rows(mom, 1, j * width, spread)
        for side in range(2):
            remote(line_out.at[j], line_in.at[j, 1 - side], sem3.at[2, j], sem3.at[3, j], neighbour(side)).start()

    def send_parts(j):
        received(line_in.at[j], sem3.at[3, j])

        def side_part(side, carry):
            def store(row, value):
                put_rows(part_out.at[j, side], row, 0, value)

            accumulate(j, wslot, own_slots + side * far_slots, far_slots, 7, line_in[j, side, 0], line_in[j, side, 1], store)
            return carry

        def send(side):
            remote(part_out.at[j, side], part_in.at[j, side], sem3.at[4, j], sem3.at[5, j], neighbour(side)).start()

        def store(row, value):
            put_rows(dens, row, j * width, value)

        lax.fori_loop(0, 2, side_part, 0)
        send(0)
        accumulate(j, wslot, 0, own_slots, 8, line_own[j, 0], line_own[j, 1], store)
        send(1)

    def add_parts(j):
        received(part_in.at[j], sem3.at[5, j])
        lanes = pl.ds(j * width, width)
        dens[:, lanes] = mom[1:2, lanes] * (dens[:, lanes] + part_in[j, 0] + part_in[j, 1])

    def evaluate(j):
        centre, second = moments(j, wnorm, 0, n_cfg)
        spread = jnp.sqrt(second)
        put_rows(mom, 0, j * width, centre)
        put_rows(mom, 1, j * width, spread)

        def store(row, value):
            put_rows(dens, row, j * width, spread * value)

        accumulate(j, wnorm, 0, n_cfg, 8, centre, spread, store)

    def ahead(j):
        return [j + AHEAD] if j + AHEAD < CHUNKS else []

    second_hop(0, range(1, AHEAD + 1))
    send_weights()
    second_hop(1, ahead(1))
    normalize_weights()
    for step in range(1, CHUNKS + 1):
        wait_blocks(step - 1)
        if step - 1 < MERGED:
            send_stats(step - 1)
        if 0 <= step - 2 < MERGED:
            merge_stats(step - 2)
        if step + 1 < CHUNKS:
            second_hop(step + 1, ahead(step + 1))
        if 0 <= step - 3 < MERGED:
            send_parts(step - 3)
        if step - 1 >= MERGED:
            evaluate(step - 1)
        if 0 <= step - 5 < MERGED:
            add_parts(step - 5)
    for j in range(CHUNKS - 4, MERGED):
        add_parts(j)

    def finish_first(i, carry):
        for j in range(CHUNKS):
            for a in range(2):
                pltpu.make_async_copy(relay.at[j, 0, :, :, 0, a], relay.at[j, 0, :, :, 0, a], sem1.at[j]).wait()
        return carry

    lax.fori_loop(1, n_row, finish_first, 0)
    for j in range(CHUNKS):
        count = n_cfg - NX * (3 if j < MERGED else 1)
        received(buf.at[j, pl.ds(0, count)], sem2.at[0, j])
    for j in range(MERGED):
        received(stat_out.at[j], sem3.at[0, j])
        received(line_in.at[j], sem3.at[2, j])
        received(part_out.at[j], sem3.at[4, j])

    pltpu.make_async_copy(wbuf.at[pl.ds(0, n_cfg - NX)], wbuf.at[pl.ds(0, n_cfg - NX)], wsem.at[2]).wait()


def per_device(latent_mode, latent_var, config_weight, grid_offset):
    n_cfg = lax.axis_size("cfg")
    n_lat = lax.axis_size("lat")
    own, width = latent_mode.shape
    grid = grid_offset.shape[0]
    lat_dev = width // n_cfg
    block = own * lat_dev // LANES
    size = block // CHUNKS

    def rows(a):
        a = a.reshape(own, width // LANES, LANES).transpose(1, 0, 2)
        return a.reshape(n_cfg // n_lat // (NX * NY), NX, NY, n_lat, block, LANES)

    vmem = pl.BlockSpec(memory_space=pltpu.VMEM)
    in_hbm = functools.partial(pltpu.with_memory_space_constraint, memory_space=pltpu.HBM)
    smem = pl.BlockSpec(memory_space=pltpu.SMEM)
    hbm = pl.BlockSpec(memory_space=pltpu.HBM)
    return pl.pallas_call(
        functools.partial(kernel, n_lat),
        out_shape=(
            jax.ShapeDtypeStruct((grid, lat_dev), jnp.float32),
            jax.ShapeDtypeStruct((2, lat_dev), jnp.float32),
        ),
        in_specs=[hbm, hbm, smem, smem],
        out_specs=(vmem, vmem),
        scratch_shapes=[
            pltpu.VMEM((CHUNKS, n_lat, NZ // n_lat, NY, NX, 2, size, LANES), jnp.float32),
            pltpu.VMEM((CHUNKS, n_cfg, 2, size, LANES), jnp.float32),
            pltpu.VMEM((NX, own, LANES), jnp.float32),
            pltpu.VMEM((n_cfg, own, LANES), jnp.float32),
            pltpu.VMEM((n_cfg, 8, LANES), jnp.float32),
            pltpu.VMEM((n_cfg, 8, LANES), jnp.float32),
            pltpu.VMEM((2, n_cfg, 8, LANES), jnp.float32),
            pltpu.VMEM((3, 8, LANES), jnp.float32),
            pltpu.VMEM((MERGED, 2, 8, LANES), jnp.float32),
            pltpu.VMEM((MERGED, 2, 2, 8, LANES), jnp.float32),
            pltpu.VMEM((MERGED, 2, 2, 8, LANES), jnp.float32),
            pltpu.VMEM((MERGED, 2, 8, LANES), jnp.float32),
            pltpu.VMEM((MERGED, 2, 8, LANES), jnp.float32),
            pltpu.VMEM((MERGED, 2, 2, 8, LANES), jnp.float32),
            pltpu.VMEM((MERGED, 2, grid, lat_dev // CHUNKS), jnp.float32),
            pltpu.VMEM((MERGED, 2, grid, lat_dev // CHUNKS), jnp.float32),
            pltpu.SemaphoreType.DMA((CHUNKS,)),
            pltpu.SemaphoreType.DMA((CHUNKS, n_lat)),
            pltpu.SemaphoreType.DMA((2, CHUNKS)),
            pltpu.SemaphoreType.DMA((4,)),
            pltpu.SemaphoreType.DMA((6, MERGED)),
        ],
        compiler_params=pltpu.CompilerParams(collective_id=0, has_side_effects=True, vmem_limit_bytes=52 * 1024 * 1024),
        name="mixture",
    )(rows(latent_mode), rows(latent_var), in_hbm(config_weight), in_hbm(grid_offset))


def solution(mesh):
    return jax.shard_map(
        per_device,
        mesh=mesh,
        in_specs=(P("cfg", "lat"), P("cfg", "lat"), P("cfg"), P()),
        out_specs=(P(None, ("cfg", "lat")), P(None, ("cfg", "lat"))),
        check_vma=False,
    )
```

time: 119 us -> 107 us (0.90)
  Pallas kernels: 116 us -> 105 us
  local copies, waits for them, and re-layouts: 2.89 us -> 1.59 us
    pallas_call x1, Pallas kernels: 116 us -> 105 us  [per_device(): pl.pallas_call(functools.partial(kernel, n_lat), out_shape=(jax.ShapeDtyp...]
    unnamed x6 -> x2, local copies, waits for them, and re-layouts: 2.89 us -> 1.59 us
where the time goes in v5:
time: 107 us
  Pallas kernels  105 us (98%)
  local copies, waits for them, and re-layouts  1.59 us (1%)
    pallas_call x1, Pallas kernels, per_device(): pl.pallas_call(functools.partial(kernel, n_lat), out_shape=(jax.ShapeDtyp...  105 us

profile of v5, /device:TPU:1, one launch (start us, length us, event | category | flops | bytes accessed | tf_op | source)
XLA Modules:
  0.0 107.0 jit_solution(15005677163434105101)
XLA Ops:
  0.6 104.8 %mixture.1 = (f32[64,4096]{1,0:T(8,128)S(1)}, f32[2,4096]{1,0:T(2,128)S(1)}) custom-call(f32[2,2,4,4,64,128]{5,4,3,2,1,0:T(8,128)} %bitcast.10, f32[2,2,4,4,64,128]{5,4,3,2,1,0:T(8,128)} %bitcast.11, f32[2]{0:T(128)} %weight.1, f32[64]{0:T(128)} %offset.1), custom_call_target="tpu_custom_call" | custom-call | tf_op jit(solution)/shard_map/mixture/pallas_call | solution.py:413
  105.5 1.0 copy.10
  106.4 0.6 copy.11

commit v6 on v5

--- a/solution.py
+++ b/solution.py
@@ -16,7 +16,7 @@
 GROUP = 16
 UNROLL = 4
 MERGED = 5
-DIST_ORDER = (4, 2, 6, 3, 5, 1, 7, 0)
+DIST_ORDER = (4, 3, 5, 2, 6, 1, 7, 0)
 LOG2E = 1.4426950408889634
 NZ, NX, NY = 8, 2, 4
 LAT_ORDER = (0, 2, 1, 3)
@@ -27,7 +27,7 @@
     return x + jnp.where(even, pltpu.roll(x, 7, 0), pltpu.roll(x, 1, 0))
 
 
-def kernel(n_lat, mode, var, weight, offset, dens, mom, relay, buf, wpair, wbuf, wnorm, wslot, coef, share_w, stat_own, stat_out, stat_in,
+def kernel(n_lat, mode, var, weight_hbm, offset_hbm, dens, mom, weight, offset, small_sem, relay, buf, wpair, wbuf, wnorm, wslot, coef, share_w, stat_own, stat_out, stat_in,
            line_own, line_out, line_in, part_out, part_in, sem1, sem1r, sem2, wsem, sem3):
     c = lax.axis_index("cfg")
     l = lax.axis_index("lat")
@@ -135,21 +135,17 @@
                     first_hop_send(f, *row_peer(peer))
                 merge_send(j, d, dy)
             return
-        share = (n_plane - 1) // (n_row - 1)
-        for i in range(n_row - 1):
-            for f in following:
-                first_hop_send(f, *row_peer(i))
-
-            def body(k, carry):
-                tz, ty, _ = plane_peer(k)
-                second_hop_send(j, tz, ty)
-                return carry
-
-            lax.fori_loop(i * share + 1, n_plane if i == n_row - 2 else (i + 1) * share + 1, body, 0)
+        for n, (dy, d) in enumerate((dy, d) for dy in range(NY) for d in DIST_ORDER):
+            if n % 2 == 0 and n // 2 < len(pairs):
+                f, peer = pairs[n // 2]
+                first_hop_send(f, *row_peer(peer))
+            if (dy, d) != (0, 0):
+                second_hop_send(j, lax.rem(z + NZ - d, NZ), lax.rem(y + dy, NY))
         buf[j, mine] = block(j, z, y)[...]
 
-    for r in range(2):
-        wpair[xl, r : r + 1, :] = jnp.full((1, LANES), weight[r], jnp.float32)
+    small = [pltpu.make_async_copy(weight_hbm, weight, small_sem.at[0]), pltpu.make_async_copy(offset_hbm, offset, small_sem.at[1])]
+    for copy in small:
+        copy.start()
 
     barrier = pltpu.get_barrier_semaphore()
 
@@ -162,6 +158,10 @@
         tx, tl = row_peer(i)
         pl.semaphore_signal(barrier, inc=1, device_id=(z * NX * NY + tx * NY + y, tl), device_id_type=MESH)
     first_hop_own(0)
+    for copy in small:
+        copy.wait()
+    for r in range(2):
+        wpair[xl, r : r + 1, :] = jnp.full((1, LANES), weight[r], jnp.float32)
     pl.semaphore_wait(barrier, n_plane + n_row - 2)
 
     for i in range(n_row - 1):
@@ -232,14 +232,14 @@
         def first(s, acc):
             return acc[0] + w_ref[low + s] * buf[j, low + s, 0], acc[1] + w_ref[low + s]
 
-        total, weight_sum = lax.fori_loop(0, count, first, (zero, zero), unroll=4)
+        total, weight_sum = lax.fori_loop(0, count, first, (zero, zero), unroll=True if count == 8 else 14 if count == 28 else 16)
         mean = pair_sum(total, even) / pair_sum(weight_sum, even)
 
         def second(s, acc):
             dev = buf[j, low + s, 0] - mean
             return acc + w_ref[low + s] * (buf[j, low + s, 1] + dev * dev)
 
-        return mean, pair_sum(lax.fori_loop(0, count, second, zero, unroll=4), even)
+        return mean, pair_sum(lax.fori_loop(0, count, second, zero, unroll=True if count == 8 else 14 if count == 28 else 16), even)
 
     def accumulate(j, w_ref, low, count, unroll, centre, spread, store):
         def prepare(s, carry):
@@ -248,7 +248,7 @@
             coef[1, s] = w_ref[low + s] * lax.rsqrt((2.0 * math.pi) * var_s)
             return carry
 
-        lax.fori_loop(0, count, prepare, 0, unroll=4)
+        lax.fori_loop(0, count, prepare, 0, unroll=True if count == 8 else 7 if count == 28 else 16)
 
         for base in range(0, dens.shape[0], GROUP):
             points = [centre + offset[base + g] * spread for g in range(GROUP)]
@@ -265,6 +265,9 @@
             for g in range(GROUP):
                 store(base + g, pair_sum(accs[g], even))
 
+    def unpaired(x):
+        return jnp.where(even, x, pltpu.roll(x, 1, 0)), jnp.where(even, pltpu.roll(x, 7, 0), x)
+
     tiles = 4
     width = tiles * LANES
 
@@ -285,8 +288,7 @@
     def send_stats(j):
         def side_stats(side, carry):
             mean, second = moments(j, wslot, own_slots + side * far_slots, far_slots)
-            stat_out[j, side, 0] = mean
-            stat_out[j, side, 1] = second
+            stat_out[j, side] = jnp.where(even, mean, second)
             return carry
 
         lax.fori_loop(0, 2, side_stats, 0)
@@ -298,17 +300,18 @@
 
     def merge_stats(j):
         received(stat_in.at[j], sem3.at[1, j])
-        means = [stat_own[j, 0], stat_in[j, 0, 0], stat_in[j, 1, 0]]
-        seconds = [stat_own[j, 1], stat_in[j, 0, 1], stat_in[j, 1, 1]]
+        pairs = [unpaired(stat_in[j, side]) for side in range(2)]
+        means = [stat_own[j, 0]] + [p[0] for p in pairs]
+        seconds = [stat_own[j, 1]] + [p[1] for p in pairs]
         shares = [share_w[i] for i in range(3)]
         centre = shares[0] * means[0] + shares[1] * means[1] + shares[2] * means[2]
         second = seconds[0] + seconds[1] + seconds[2]
         for share, mean in zip(shares, means):
             second = second + share * (mean - centre) * (mean - centre)
         spread = jnp.sqrt(second)
-        for ref in (line_own.at[j], line_out.at[j]):
-            ref[0] = centre
-            ref[1] = spread
+        line_out[j] = jnp.where(even, centre, spread)
+        line_own[j, 0] = centre
+        line_own[j, 1] = spread
         put_rows(mom, 0, j * width, centre)
         put_rows(mom, 1, j * width, spread)
         for side in range(2):
@@ -321,7 +324,7 @@
             def store(row, value):
                 put_rows(part_out.at[j, side], row, 0, value)
 
-            accumulate(j, wslot, own_slots + side * far_slots, far_slots, 7, line_in[j, side, 0], line_in[j, side, 1], store)
+            accumulate(j, wslot, own_slots + side * far_slots, far_slots, 7, *unpaired(line_in[j, side]), store)
             return carry
 
         def send(side):
@@ -408,7 +411,6 @@
 
     vmem = pl.BlockSpec(memory_space=pltpu.VMEM)
     in_hbm = functools.partial(pltpu.with_memory_space_constraint, memory_space=pltpu.HBM)
-    smem = pl.BlockSpec(memory_space=pltpu.SMEM)
     hbm = pl.BlockSpec(memory_space=pltpu.HBM)
     return pl.pallas_call(
         functools.partial(kernel, n_lat),
@@ -416,9 +418,12 @@
             jax.ShapeDtypeStruct((grid, lat_dev), jnp.float32),
             jax.ShapeDtypeStruct((2, lat_dev), jnp.float32),
         ),
-        in_specs=[hbm, hbm, smem, smem],
+        in_specs=[hbm, hbm, hbm, hbm],
         out_specs=(vmem, vmem),
         scratch_shapes=[
+            pltpu.SMEM((own,), jnp.float32),
+            pltpu.SMEM((grid,), jnp.float32),
+            pltpu.SemaphoreType.DMA((2,)),
             pltpu.VMEM((CHUNKS, n_lat, NZ // n_lat, NY, NX, 2, size, LANES), jnp.float32),
             pltpu.VMEM((CHUNKS, n_cfg, 2, size, LANES), jnp.float32),
             pltpu.VMEM((NX, own, LANES), jnp.float32),
@@ -428,11 +433,11 @@
             pltpu.VMEM((2, n_cfg, 8, LANES), jnp.float32),
             pltpu.VMEM((3, 8, LANES), jnp.float32),
             pltpu.VMEM((MERGED, 2, 8, LANES), jnp.float32),
-            pltpu.VMEM((MERGED, 2, 2, 8, LANES), jnp.float32),
-            pltpu.VMEM((MERGED, 2, 2, 8, LANES), jnp.float32),
             pltpu.VMEM((MERGED, 2, 8, LANES), jnp.float32),
             pltpu.VMEM((MERGED, 2, 8, LANES), jnp.float32),
-            pltpu.VMEM((MERGED, 2, 2, 8, LANES), jnp.float32),
+            pltpu.VMEM((MERGED, 2, 8, LANES), jnp.float32),
+            pltpu.VMEM((MERGED, 8, LANES), jnp.float32),
+            pltpu.VMEM((MERGED, 2, 8, LANES), jnp.float32),
             pltpu.VMEM((MERGED, 2, grid, lat_dev // CHUNKS), jnp.float32),
             pltpu.VMEM((MERGED, 2, grid, lat_dev // CHUNKS), jnp.float32),
             pltpu.SemaphoreType.DMA((CHUNKS,)),

time: 107 us -> 105 us (0.981)
  Pallas kernels: 105 us -> 102 us
    pallas_call x1, Pallas kernels: 105 us -> 102 us  [per_device(): pl.pallas_call(functools.partial(kernel, n_lat), out_shape=(jax.ShapeDtyp...]
where the time goes in v6:
time: 105 us
  Pallas kernels  102 us (97%)
  local copies, waits for them, and re-layouts  1.59 us (2%)
    pallas_call x1, Pallas kernels, per_device(): pl.pallas_call(functools.partial(kernel, n_lat), out_shape=(jax.ShapeDtyp...  102 us

profile of v6, /device:TPU:1, one launch (start us, length us, event | category | flops | bytes accessed | tf_op | source)
XLA Modules:
  0.0 104.6 jit_solution(342135995609501579)
XLA Ops:
  0.6 102.3 %mixture.1 = (f32[64,4096]{1,0:T(8,128)S(1)}, f32[2,4096]{1,0:T(2,128)S(1)}) custom-call(f32[2,2,4,4,64,128]{5,4,3,2,1,0:T(8,128)} %bitcast.10, f32[2,2,4,4,64,128]{5,4,3,2,1,0:T(8,128)} %bitcast.11, f32[2]{0:T(128)} %weight_hbm.1, f32[64]{0:T(128)} %offset_hbm.1), custom_call_target="tpu_custom_call" | custom-call | tf_op jit(solution)/shard_map/mixture/pallas_call | solution.py:415
  103.0 1.0 copy.10
  104.0 0.6 copy.11

commit v7 on v6

--- a/solution.py
+++ b/solution.py
@@ -333,9 +333,14 @@
         def store(row, value):
             put_rows(dens, row, j * width, value)
 
-        lax.fori_loop(0, 2, side_part, 0)
+        lax.fori_loop(0, 1, side_part, 0)
+        if j < 2:
+            lax.fori_loop(1, 2, side_part, 0)
+        accumulate(j, wslot, 0, own_slots, 8, line_own[j, 0], line_own[j, 1], store)
         send(0)
-        accumulate(j, wslot, 0, own_slots, 8, line_own[j, 0], line_own[j, 1], store)
+        if j >= 2:
+            lax.fori_loop(1, 2, side_part, 0)
+            add_parts(j - 2)
         send(1)
 
     def add_parts(j):
@@ -373,7 +378,7 @@
             send_parts(step - 3)
         if step - 1 >= MERGED:
             evaluate(step - 1)
-        if 0 <= step - 5 < MERGED:
+        if step == CHUNKS:
             add_parts(step - 5)
     for j in range(CHUNKS - 4, MERGED):
         add_parts(j)

time: 105 us -> 105 us (level)
  no operation moved by 1% of the time
where the time goes in v7:
time: 105 us
  Pallas kernels  102 us (97%)
  local copies, waits for them, and re-layouts  1.59 us (2%)
    pallas_call x1, Pallas kernels, per_device(): pl.pallas_call(functools.partial(kernel, n_lat), out_shape=(jax.ShapeDtyp...  102 us

profile of v7, /device:TPU:1, one launch (start us, length us, event | category | flops | bytes accessed | tf_op | source)
XLA Modules:
  0.0 104.6 jit_solution(9383382823661677039)
XLA Ops:
  0.6 102.3 %mixture.1 = (f32[64,4096]{1,0:T(8,128)S(1)}, f32[2,4096]{1,0:T(2,128)S(1)}) custom-call(f32[2,2,4,4,64,128]{5,4,3,2,1,0:T(8,128)} %bitcast.10, f32[2,2,4,4,64,128]{5,4,3,2,1,0:T(8,128)} %bitcast.11, f32[2]{0:T(128)} %weight_hbm.1, f32[64]{0:T(128)} %offset_hbm.1), custom_call_target="tpu_custom_call" | custom-call | tf_op jit(solution)/shard_map/mixture/pallas_call | solution.py:420
  103.0 1.0 copy.10
  104.0 0.6 copy.11
